TPU v7x, 32 devices: a whole 2x2x4 slice. The times are simulated.
32 devices in a mesh: dp: 16 (over z, y, core), inner: 2 (over x).
Axes of the slice: x: 2, y: 2, z: 4, core: 2. Of those that a mesh axis runs over, the one named last changes fastest.
Arguments:
- tokens: bfloat16 [65536, 768], P(('dp', 'inner')), may hold values from -6 to 6
- out_grad: bfloat16 [65536, 768], P(('dp', 'inner')), may hold values from -6 to 6
- norm1_gain: bfloat16 [768], P(('dp', 'inner')), may hold values from 0.5 to 1.5
- norm1_shift: bfloat16 [768], P(('dp', 'inner')), may hold values from -3 to 3
- qkv_weight: bfloat16 [768, 2304], P('dp', 'inner'), may hold values from -0.21875 to 0.21875
- qkv_bias: bfloat16 [2304], P(('dp', 'inner')), may hold values from -3 to 3
- proj_weight: bfloat16 [768, 768], P('dp', 'inner'), may hold values from -3 to 3
- proj_bias: bfloat16 [768], P(('dp', 'inner')), may hold values from -3 to 3
- norm2_gain: bfloat16 [768], P(('dp', 'inner')), may hold values from 0.5 to 1.5
- norm2_shift: bfloat16 [768], P(('dp', 'inner')), may hold values from -3 to 3
- up_weight: bfloat16 [768, 3072], P('dp', 'inner'), may hold values from -0.21875 to 0.21875
- up_bias: bfloat16 [3072], P(('dp', 'inner')), may hold values from -3 to 3
- down_weight: bfloat16 [3072, 768], P('dp', 'inner'), may hold values from -0.109375 to 0.109375
- down_bias: bfloat16 [768], P(('dp', 'inner')), may hold values from -3 to 3
Outputs:
- output: bfloat16 [65536, 768], P(('dp', 'inner'))
- grad_tokens: float32 [65536, 768], P(('dp', 'inner'))
- grad_norm1_gain: float32 [768], P(('dp', 'inner'))
- grad_norm1_shift: float32 [768], P(('dp', 'inner'))
- grad_qkv_weight: float32 [768, 2304], P('dp', 'inner')
- grad_qkv_bias: float32 [2304], P(('dp', 'inner'))
- grad_proj_weight: float32 [768, 768], P('dp', 'inner')
- grad_proj_bias: float32 [768], P(('dp', 'inner'))
- grad_norm2_gain: float32 [768], P(('dp', 'inner'))
- grad_norm2_shift: float32 [768], P(('dp', 'inner'))
- grad_up_weight: float32 [768, 3072], P('dp', 'inner')
- grad_up_bias: float32 [3072], P(('dp', 'inner'))
- grad_down_weight: float32 [3072, 768], P('dp', 'inner')
- grad_down_bias: float32 [768], P(('dp', 'inner'))
All inputs are finite; a program needn't handle non-finite values.
Results may differ from a plain program's by a relative error of at most 0.02.
Values may be sent and summed in bfloat16 or wider, within the bound.
A program may use at most 256 MiB of HBM per device.

v0:
```python
import jax
import jax.numpy as jnp
from jax import lax
from jax.sharding import PartitionSpec as P

D = 768
HEADS = 12
HEAD_DIM = 64
SHORT = 1024
LONG = 2048
BLOCK = 512


epsilon = 1e-05


def layer_norm(values, gain_vec, shift_vec):
    center = values - jnp.mean(values, axis=-1, keepdims=True)
    spread = jnp.mean(center * center, axis=-1, keepdims=True)
    return center * lax.rsqrt(spread + epsilon) * gain_vec + shift_vec


def gelu_tanh(values):
    return jax.nn.gelu(values, approximate=True)


def as_rows(vector):
    return vector.reshape(1, vector.shape[0])


def collect(first_m, second_m, third_m, fourth_m, fifth_m, sixth_m):
    partial_set = (
        lax.all_gather(first_m, "inner", axis=1, tiled=True),
        lax.all_gather(second_m, "inner", axis=1, tiled=True),
        lax.all_gather(third_m, "inner", axis=1, tiled=True),
        lax.all_gather(fourth_m, "inner", axis=1, tiled=True),
        lax.all_gather(fifth_m, "inner", axis=1, tiled=True),
        lax.all_gather(sixth_m, "inner", axis=1, tiled=True),
    )
    whole_set = (
        lax.all_gather(partial_set[0], "dp", axis=0, tiled=True),
        lax.all_gather(partial_set[1], "dp", axis=0, tiled=True),
        lax.all_gather(partial_set[2], "dp", axis=0, tiled=True),
        lax.all_gather(partial_set[3], "dp", axis=0, tiled=True),
        lax.all_gather(partial_set[4], "dp", axis=0, tiled=True),
        lax.all_gather(partial_set[5], "dp", axis=0, tiled=True),
    )
    return whole_set


def fetch(gain_vec, shift_vec, first_weight, first_bias, second_weight, second_bias):
    whole_set = collect(
        as_rows(gain_vec),
        as_rows(shift_vec),
        first_weight,
        as_rows(first_bias),
        second_weight,
        as_rows(second_bias),
    )
    return (
        whole_set[0].reshape(-1).astype(jnp.float32),
        whole_set[1].reshape(-1).astype(jnp.float32),
        whole_set[2],
        whole_set[3].reshape(-1),
        whole_set[4],
        whole_set[5].reshape(-1),
    )


def deliver(gain_grad, shift_grad, first_grad, first_bias_grad, second_grad, second_bias_grad):
    wide_count = lax.axis_size("dp")
    first_v = gain_grad.reshape(wide_count, -1)
    second_v = shift_grad.reshape(wide_count, -1)
    fourth_v = first_bias_grad.reshape(wide_count, -1)
    sixth_v = second_bias_grad.reshape(wide_count, -1)
    partial_set = (
        lax.psum_scatter(
            first_v.astype(jnp.bfloat16), "dp", scatter_dimension=0, tiled=True
        ).astype(jnp.float32),
        lax.psum_scatter(
            second_v.astype(jnp.bfloat16), "dp", scatter_dimension=0, tiled=True
        ).astype(jnp.float32),
        lax.psum_scatter(
            first_grad.astype(jnp.bfloat16), "dp", scatter_dimension=0, tiled=True
        ).astype(jnp.float32),
        lax.psum_scatter(
            fourth_v.astype(jnp.bfloat16), "dp", scatter_dimension=0, tiled=True
        ).astype(jnp.float32),
        lax.psum_scatter(
            second_grad.astype(jnp.bfloat16), "dp", scatter_dimension=0, tiled=True
        ).astype(jnp.float32),
        lax.psum_scatter(
            sixth_v.astype(jnp.bfloat16), "dp", scatter_dimension=0, tiled=True
        ).astype(jnp.float32),
    )
    shard_set = (
        lax.psum_scatter(
            partial_set[0].astype(jnp.bfloat16), "inner", scatter_dimension=1, tiled=True
        ).astype(jnp.float32),
        lax.psum_scatter(
            partial_set[1].astype(jnp.bfloat16), "inner", scatter_dimension=1, tiled=True
        ).astype(jnp.float32),
        lax.psum_scatter(
            partial_set[2].astype(jnp.bfloat16), "inner", scatter_dimension=1, tiled=True
        ).astype(jnp.float32),
        lax.psum_scatter(
            partial_set[3].astype(jnp.bfloat16), "inner", scatter_dimension=1, tiled=True
        ).astype(jnp.float32),
        lax.psum_scatter(
            partial_set[4].astype(jnp.bfloat16), "inner", scatter_dimension=1, tiled=True
        ).astype(jnp.float32),
        lax.psum_scatter(
            partial_set[5].astype(jnp.bfloat16), "inner", scatter_dimension=1, tiled=True
        ).astype(jnp.float32),
    )
    return (
        shard_set[0].reshape(-1),
        shard_set[1].reshape(-1),
        shard_set[2],
        shard_set[3].reshape(-1),
        shard_set[4],
        shard_set[5].reshape(-1),
    )


def allowed(first_row, rows, width, seq_len):
    row_pos = first_row + lax.broadcasted_iota(jnp.int32, (rows, width), 0)
    col_pos = lax.broadcasted_iota(jnp.int32, (rows, width), 1)
    return (col_pos <= row_pos) & (col_pos // seq_len == row_pos // seq_len)


def forward_head(queries, keys_in, values_in, seq_len, score_scale):
    outputs = []
    totals = []
    for first_row in range(0, queries.shape[0], BLOCK):
        stop_row = first_row + BLOCK
        scores = (
            jnp.einsum(
                "qd,kd->qk",
                queries[first_row:stop_row],
                keys_in[:stop_row],
                preferred_element_type=jnp.float32,
            )
            * score_scale
        )
        allowed_mask = allowed(first_row, BLOCK, stop_row, seq_len)
        magnitudes = jnp.where(allowed_mask, jnp.abs(scores), -1e30)
        row_peak = jnp.max(magnitudes, axis=1, keepdims=True)
        exponents = jnp.exp(magnitudes - row_peak)
        expo_sum = jnp.sum(exponents, axis=1, keepdims=True)
        weights = (jnp.sign(scores) * (exponents / expo_sum)).astype(jnp.bfloat16)
        outputs.append(jnp.dot(weights, values_in[:stop_row], preferred_element_type=jnp.float32))
        totals.append(row_peak[:, 0] + jnp.log(expo_sum[:, 0]))
    return (jnp.concatenate(outputs, 0), jnp.concatenate(totals, 0))


def backward_head(queries, keys_in, values_in, grad_out, log_totals, seq_len, score_scale):
    rows_all = queries.shape[0]
    grad_keys = jnp.zeros((rows_all, queries.shape[1]), jnp.float32)
    grad_values = jnp.zeros((rows_all, queries.shape[1]), jnp.float32)
    grad_queries = []
    for first_row in range(0, rows_all, BLOCK):
        stop_row = first_row + BLOCK
        query_block = queries[first_row:stop_row]
        grad_block = grad_out[first_row:stop_row]
        scores = (
            jnp.einsum(
                "qd,kd->qk", query_block, keys_in[:stop_row], preferred_element_type=jnp.float32
            )
            * score_scale
        )
        allowed_mask = allowed(first_row, BLOCK, stop_row, seq_len)
        probabilities = jnp.where(
            allowed_mask, jnp.exp(jnp.abs(scores) - log_totals[first_row:stop_row, None]), 0.0
        )
        signed = jnp.sign(scores) * probabilities
        grad_weights = jnp.einsum(
            "qd,kd->qk", grad_block, values_in[:stop_row], preferred_element_type=jnp.float32
        )
        row_inner = jnp.sum(signed * grad_weights, axis=1, keepdims=True)
        grad_scores = (probabilities * grad_weights - signed * row_inner).astype(jnp.bfloat16)
        grad_values = grad_values.at[:stop_row].add(
            jnp.einsum(
                "qk,qd->kd",
                signed.astype(jnp.bfloat16),
                grad_block,
                preferred_element_type=jnp.float32,
            )
        )
        grad_queries.append(
            jnp.dot(grad_scores, keys_in[:stop_row], preferred_element_type=jnp.float32)
            * score_scale
        )
        grad_keys = grad_keys.at[:stop_row].add(
            jnp.einsum("qk,qd->kd", grad_scores, query_block, preferred_element_type=jnp.float32)
            * score_scale
        )
    return (jnp.concatenate(grad_queries, 0), grad_keys, grad_values)


def on_device(
    tokens,
    out_grad,
    norm1_gain,
    norm1_shift,
    qkv_weight,
    qkv_bias,
    proj_weight,
    proj_bias,
    norm2_gain,
    norm2_shift,
    up_weight,
    up_bias,
    down_weight,
    down_bias,
):
    row_count = tokens.shape[0]
    wide_count = lax.axis_size("dp")
    seq_len = jnp.where(lax.axis_index("dp") < wide_count // 2, SHORT, LONG).astype(jnp.int32)
    score_scale = HEAD_DIM ** (-0.5)
    attn_params = fetch(norm1_gain, norm1_shift, qkv_weight, qkv_bias, proj_weight, proj_bias)
    resid = tokens.astype(jnp.float32)
    normed_low = layer_norm(resid, attn_params[0], attn_params[1]).astype(jnp.bfloat16)
    mixed = (
        jnp.dot(normed_low, attn_params[2], preferred_element_type=jnp.float32) + attn_params[3]
    ).astype(jnp.bfloat16)
    split_heads = mixed.reshape(row_count, 3, HEADS, HEAD_DIM).transpose(1, 2, 0, 3)
    head_outputs, log_totals = lax.map(
        lambda member: forward_head(member[0], member[1], member[2], seq_len, score_scale),
        (split_heads[0], split_heads[1], split_heads[2]),
    )
    attended = head_outputs.transpose(1, 0, 2).reshape(row_count, D).astype(jnp.bfloat16)
    middle = (
        resid
        + jnp.dot(attended, attn_params[4], preferred_element_type=jnp.float32)
        + attn_params[5]
    )
    mlp_params = fetch(norm2_gain, norm2_shift, up_weight, up_bias, down_weight, down_bias)
    normed_two = layer_norm(middle, mlp_params[0], mlp_params[1]).astype(jnp.bfloat16)
    pre_act = jnp.dot(normed_two, mlp_params[2], preferred_element_type=jnp.float32) + mlp_params[3]
    active = gelu_tanh(pre_act).astype(jnp.bfloat16)
    final_rows = (
        middle + jnp.dot(active, mlp_params[4], preferred_element_type=jnp.float32) + mlp_params[5]
    )
    output = final_rows.astype(jnp.bfloat16)
    mlp_back = fetch(norm2_gain, norm2_shift, up_weight, up_bias, down_weight, down_bias)
    grad_final = out_grad.astype(jnp.float32)
    grad_down_bias = jnp.sum(grad_final, axis=0)
    grad_down = jnp.einsum("ti,td->id", active, out_grad, preferred_element_type=jnp.float32)
    grad_active = jnp.einsum("td,id->ti", out_grad, mlp_back[4], preferred_element_type=jnp.float32)
    _, gelu_pull = jax.vjp(gelu_tanh, pre_act)
    grad_pre = gelu_pull(grad_active)[0].astype(jnp.bfloat16)
    grad_up_bias = jnp.sum(grad_pre.astype(jnp.float32), axis=0)
    grad_up = jnp.einsum("td,ti->di", normed_two, grad_pre, preferred_element_type=jnp.float32)
    grad_normed_two = jnp.einsum(
        "ti,di->td", grad_pre, mlp_back[2], preferred_element_type=jnp.float32
    )
    _, norm_two_pull = jax.vjp(layer_norm, middle, mlp_back[0], mlp_back[1])
    grad_middle_norm, grad_gain_two, grad_shift_two = norm_two_pull(grad_normed_two)
    grad_middle = grad_final + grad_middle_norm
    mlp_shards = deliver(
        grad_gain_two, grad_shift_two, grad_up, grad_up_bias, grad_down, grad_down_bias
    )
    attn_back = fetch(norm1_gain, norm1_shift, qkv_weight, qkv_bias, proj_weight, proj_bias)
    grad_proj_in = grad_middle.astype(jnp.bfloat16)
    grad_proj_bias = jnp.sum(grad_proj_in.astype(jnp.float32), axis=0)
    grad_proj = jnp.einsum("td,te->de", attended, grad_proj_in, preferred_element_type=jnp.float32)
    grad_attended = jnp.einsum(
        "te,de->td", grad_proj_in, attn_back[4], preferred_element_type=jnp.float32
    ).astype(jnp.bfloat16)
    grad_heads = grad_attended.reshape(row_count, HEADS, HEAD_DIM).transpose(1, 0, 2)
    grad_queries, grad_keys, grad_values = lax.map(
        lambda member: backward_head(
            member[0], member[1], member[2], member[3], member[4], seq_len, score_scale
        ),
        (split_heads[0], split_heads[1], split_heads[2], grad_heads, log_totals),
    )
    grad_mixed = (
        jnp.stack((grad_queries, grad_keys, grad_values))
        .transpose(2, 0, 1, 3)
        .reshape(row_count, 3 * D)
        .astype(jnp.bfloat16)
    )
    grad_qkv_bias = jnp.sum(grad_mixed.astype(jnp.float32), axis=0)
    grad_qkv = jnp.einsum("td,te->de", normed_low, grad_mixed, preferred_element_type=jnp.float32)
    grad_normed_one = jnp.einsum(
        "te,de->td", grad_mixed, attn_back[2], preferred_element_type=jnp.float32
    )
    _, norm_one_pull = jax.vjp(layer_norm, resid, attn_back[0], attn_back[1])
    grad_resid_norm, grad_gain_one, grad_shift_one = norm_one_pull(grad_normed_one)
    grad_input = grad_middle + grad_resid_norm
    attn_shards = deliver(
        grad_gain_one, grad_shift_one, grad_qkv, grad_qkv_bias, grad_proj, grad_proj_bias
    )
    return (
        output,
        grad_input,
        attn_shards[0],
        attn_shards[1],
        attn_shards[2],
        attn_shards[3],
        attn_shards[4],
        attn_shards[5],
        mlp_shards[0],
        mlp_shards[1],
        mlp_shards[2],
        mlp_shards[3],
        mlp_shards[4],
        mlp_shards[5],
    )


def solution(mesh):
    return jax.shard_map(
        on_device,
        mesh=mesh,
        in_specs=(
            P(("dp", "inner"), None),
            P(("dp", "inner"), None),
            P(("dp", "inner")),
            P(("dp", "inner")),
            P("dp", "inner"),
            P(("dp", "inner")),
            P("dp", "inner"),
            P(("dp", "inner")),
            P(("dp", "inner")),
            P(("dp", "inner")),
            P("dp", "inner"),
            P(("dp", "inner")),
            P("dp", "inner"),
            P(("dp", "inner")),
        ),
        out_specs=(
            P(("dp", "inner"), None),
            P(("dp", "inner"), None),
            P(("dp", "inner")),
            P(("dp", "inner")),
            P("dp", "inner"),
            P(("dp", "inner")),
            P("dp", "inner"),
            P(("dp", "inner")),
            P(("dp", "inner")),
            P(("dp", "inner")),
            P("dp", "inner"),
            P(("dp", "inner")),
            P("dp", "inner"),
            P(("dp", "inner")),
        ),
        check_vma=False,
    )
```

profile of v0, /device:TPU:0, one launch (start us, length us, event | category | flops | bytes accessed | tf_op | source)
XLA Modules:
  0.0 1781.2 jit_solution(3642825452598079560)
XLA Ops:
  7.2 8.6 all_gather.88
  15.9 4.9 all_gather.92
  20.9 7.0 all_gather.100
  28.0 6.3 all_gather.104
  46.5 5.4 all-reduce.36
  53.3 58.9 %all-reduce.34 = (bf16[2304]{0:T(1024)(128)(2,1)S(1)}, bf16[768]{0:T(1024)(128)(2,1)S(1)}, bf16[768]{0:T(1024)(128)(2,1)S(1)}, bf16[768]{0:T(1024)(128)(2,1)S(1)...) all-reduce(bf16[2304]{0:T(1024)(128)(2,1)S(1)} %dynamic-update-slic, ...), channel_id=7, replica_groups=mesh['dp'=16,'inner'=2] {'dp'}, use_global_device_ids=true, to_apply=%add.7 | all-reduce | flops 9216 | bytes 36864
  119.8 4.7 copy.62
  124.6 12.4 add_convert_fusion
  137.0 12.8 copy.57
  149.8 6.0 slice_bitcast_fusion
  155.8 6.6 copy.58
  162.4 6.6 copy.59
  175.6 425.7 %while.42 = (s32[]{:T(128)}, bf16[12,2048,64]{1,2,0:T(8,128)(2,1)}, f32[12,2048]{1,0:T(8,128)S(1)}, bf16[12,2048,64]{2,1,0:T(8,128)(2,1)}, bf16[12,2048,64]{2,1,...) while((s32[]{:T(128)}, bf16[12,2048,64]{1,2,0:T(8,128)(2,1)}, ...), condition=%wide.region_11.12_spmd, body=%wide.region_2.11_spmd.sunk | while | flops 753985024 | bytes 111265712 | solution.py:228
  601.4 5.2 fusion.178
  610.0 27.1 %multiply_convert_fusion.8 = (bf16[2048,3072]{1,0:T(8,128)(2,1)}, f32[2048,3072]{1,0:T(8,128)}) fusion(f32[3072]{0:T(1024)S(1)} %copy-done.34, bf16[768,3072]{1,0:T(8,128)(2,1)} %all-gather.25.cloned.1.call-done, f32[2048,768]{0,1:T(8,128)} %copy-done.8, f32[768]{0:T(1024)S(1)} %copy-done.40, f32[768]{0:T(1024)S(1)} %copy-done.32, f32[2048]{0:T(1024)S(1)} %fusion.154, ...), kind=kOutput, calls=%fused_computation.280 | convolution fusion | flops 9734455296 | bytes 48793600 | tf_op jit(solution)/shard_map/dot_general | solution.py:240
  637.1 29.9 %fusion.181 = (bf16[3072]{0:T(1024)(128)(2,1)}, bf16[2048,3072]{1,0:T(8,128)(2,1)}) fusion(f32[2048,3072]{1,0:T(8,128)} %get-tuple-element.669, f32[3072]{0:T(1024)S(1)} %copy-done.34, bf16[2048,768]{1,0:T(8,128)(2,1)S(1)} %copy-done.15, bf16[3072,768]{1,0:T(8,128)(2,1)} %all-gather.27.cloned.1.call-done), kind=kOutput, calls=%fused_computation.366 | convolution fusion | flops 9802085376 | bytes 45631488 | tf_op jit(solution)/shard_map/td,id->ti/dot_general | solution.py:250
  667.0 15.2 fusion.180
  682.2 6.7 copy.63
  689.0 6.9 multiply_reduce_fusion.4
  701.8 5.5 convolution_convert_fusion.4
  707.3 5.2 convolution_convert_fusion.3
  712.5 6.6 copy.64
  725.3 690.3 %while.43 = (s32[]{:T(128)}, bf16[12,2048,64]{1,2,0:T(8,128)(2,1)}, bf16[12,2048,64]{1,2,0:T(8,128)(2,1)}, bf16[12,2048,64]{1,2,0:T(8,128)(2,1)}, s32[]{:T(128)}...) while((s32[]{:T(128)}, bf16[12,2048,64]{1,2,0:T(8,128)(2,1)}, ...), condition=%wide.region_21.22_spmd, body=%wide.region_16.21_spmd.sunk | while | flops 1782763008 | bytes 92101936 | solution.py:272
  778.2 4.7 fusion.313
  835.7 4.7 fusion.313
  893.2 4.7 fusion.313
  950.7 4.7 fusion.313
  1008.2 4.7 fusion.313
  1065.6 4.7 fusion.313
  1180.6 4.7 fusion.313
  1410.5 4.7 fusion.313
  1415.7 5.3 fusion.174
  1424.7 9.6 convolution_convert_fusion.2
  1434.3 15.4 convolution_convert_fusion
  1450.5 16.5 convolution_convert_fusion.1
  1471.1 12.9 fusion.179
  1484.0 6.7 copy.68
  1499.5 58.5 %all-reduce.33 = (bf16[768]{0:T(1024)(128)(2,1)S(1)}, bf16[16,48]{1,0:T(8,128)(2,1)S(1)}, bf16[16,48]{1,0:T(8,128)(2,1)S(1)}, bf16[16,144]{1,0:T(8,128)(2,1)S(1)...) all-reduce(bf16[768]{0:T(1024)(128)(2,1)S(1)} %dynamic-update-slice, ...), channel_id=17, replica_groups=mesh['dp'=16,'inner'=2] {'dp'}, use_global_device_ids=true, to_apply=%add.17 | all-reduce | flops 10752 | bytes 43008
  1559.6 17.5 add_convert_fusion.1
  1578.8 8.7 add_add_fusion.2
  1592.3 28.7 %reduce-scatter.33.cloned.1.call-done = bf16[192,768]{1,0:T(8,128)(2,1)} async-done(((bf16[3072,768]{1,0:T(8,128)(2,1)}), bf16[192,768]{1,0:T(8,128)(2,1)}) %reduce-scatter.33.cloned.1.call-update) | async-done | bytes 294928 | tf_op jit(solution)/shard_map/reduce_scatter | solution.py:89
  1624.9 4.9 all-reduce.35
  1631.6 68.1 %reduce-scatter.29.cloned.1.call-done = bf16[48,3072]{1,0:T(8,128)(2,1)} async-done(((bf16[768,3072]{1,0:T(8,128)(2,1)}), bf16[48,3072]{1,0:T(8,128)(2,1)}) %reduce-scatter.29.cloned.1.call-update) | async-done | bytes 294928 | tf_op jit(solution)/shard_map/reduce_scatter | solution.py:83
  1700.3 6.7 copy.72
  1713.0 12.4 reduce-scatter.37.cloned.1.call-done
  1727.0 16.0 reduce-scatter.35.cloned.1.call-done
  1744.9 13.5 reduce-scatter.41.cloned.1.call-done
  1760.2 12.6 reduce-scatter.31.cloned.1.call-done
  (1301 shorter events, 1154.6 us)
Async XLA Ops:
  7.2 117.4 %all-gather.21.cloned.1.call-start = ((), (), s32[]{:S(2)}) async-start(), calls=%async_computation.9 | async-start | bytes 3760128 | tf_op jit(solution)/shard_map/all_gather | solution.py:43
  15.8 585.5 %all-gather.23.cloned.1.call-start = ((), (), s32[]{:S(2)}) async-start(), calls=%async_computation.10 | async-start | bytes 1253376 | tf_op jit(solution)/shard_map/all_gather | solution.py:45
  20.8 589.1 %all-gather.25.cloned.1.call-start = ((), (), s32[]{:S(2)}) async-start(), calls=%async_computation.11 | async-start | bytes 5013504 | tf_op jit(solution)/shard_map/all_gather | solution.py:43
  27.9 609.1 %all-gather.27.cloned.1.call-start = ((), (), s32[]{:S(2)}) async-start(), calls=%async_computation.12 | async-start | bytes 5013504 | tf_op jit(solution)/shard_map/all_gather | solution.py:45
  34.3 1542.7 %reduce-scatter.27.cloned.1.call-start = ((), (), s32[]{:S(2)}) async-start(), calls=%async_computation.14 | async-start | bytes 1253376 | tf_op jit(solution)/shard_map/reduce_scatter | solution.py:89
  112.2 12.4 copy-start.30
  112.2 12.4 copy-start.38
  115.5 9.1 copy-start
  116.0 8.6 copy-start.18
  117.5 19.6 %copy-start.22 = (f32[2048]{0:T(1024)}, f32[2048]{0:T(1024)S(1)}, u32[]{:S(2)}) copy-start(f32[2048]{0:T(1024)S(1)} %fusion.153) | copy-start | bytes 24580
  175.6 425.8 %copy-start.1 = (bf16[2048,768]{0,1:T(8,128)(2,1)S(1)}, bf16[2048,768]{0,1:T(8,128)(2,1)}, u32[]{:S(2)}) copy-start(bf16[2048,768]{0,1:T(8,128)(2,1)} %copy-done) | copy-start | bytes 9437188
  175.6 425.8 %copy-start.42 = (f32[768]{0:T(1024)S(1)}, f32[768]{0:T(1024)}, u32[]{:S(2)}) copy-start(f32[768]{0:T(1024)} %convert_element_type.379) | copy-start | bytes 9220
  197.0 3.7 copy-start.7
  232.5 3.7 copy-start.7
  267.9 3.7 copy-start.7
  303.3 3.7 copy-start.7
  338.8 3.7 copy-start.7
  374.2 3.7 copy-start.7
  409.6 3.7 copy-start.7
  445.0 3.7 copy-start.7
  515.9 3.7 copy-start.7
  551.3 3.7 copy-start.7
  606.7 89.2 %copy-start.20 = (f32[2048]{0:T(1024)}, f32[2048]{0:T(1024)S(1)}, u32[]{:S(2)}) copy-start(f32[2048]{0:T(1024)S(1)} %broadcast_multiply_fusion) | copy-start | bytes 24580
  609.9 85.9 %copy-start.28 = (f32[2048]{0:T(1024)}, f32[2048]{0:T(1024)S(1)}, u32[]{:S(2)}) copy-start(f32[2048]{0:T(1024)S(1)} %fusion.154) | copy-start | bytes 24580
  610.0 27.1 %copy-start.15 = (bf16[2048,768]{1,0:T(8,128)(2,1)S(1)}, bf16[2048,768]{1,0:T(8,128)(2,1)}, u32[]{:S(2)}) copy-start(bf16[2048,768]{1,0:T(8,128)(2,1)} %param.39) | copy-start | bytes 9437188
  637.1 30.0 %copy-start.44 = (bf16[768,3072]{1,0:T(8,128)(2,1)S(1)}, bf16[768,3072]{1,0:T(8,128)(2,1)}, u32[]{:S(2)}) copy-start(bf16[768,3072]{1,0:T(8,128)(2,1)} %all-gather.25.cloned.1.call-done) | copy-start | bytes 14155780
  682.2 13.7 slice-start
  689.0 7.0 slice-start.1
  689.0 7.7 copy-start.10
  1415.6 171.9 %reduce-scatter.25.cloned.1.call-start = ((), (), s32[]{:S(2)}) async-start(), calls=%async_computation.13 | async-start | bytes 3760128 | tf_op jit(solution)/shard_map/reduce_scatter | solution.py:83
  1415.7 9.0 copy-start.2
  1415.7 9.0 copy-start.19
  1415.7 9.0 copy-start.23
  1415.7 9.0 copy-start.31
  1415.7 9.0 copy-start.39
  1434.3 186.7 %reduce-scatter.33.cloned.1.call-start = ((), (), s32[]{:S(2)}) async-start(), calls=%async_computation.17 | async-start | bytes 5013504 | tf_op jit(solution)/shard_map/reduce_scatter | solution.py:89
  1449.8 249.9 %reduce-scatter.29.cloned.1.call-start = ((), (), s32[]{:S(2)}) async-start(), calls=%async_computation.15 | async-start | bytes 5013504 | tf_op jit(solution)/shard_map/reduce_scatter | solution.py:83
  1467.0 3.9 copy-start.45
  1467.0 244.6 %reduce-scatter.39.cloned.1.call-start = ((), (), s32[]{:S(2)}) async-start(), calls=%async_computation.20 | async-start | bytes 73728
  1490.8 4.2 copy-start.27
  1490.8 4.9 copy-start.5
  1495.7 3.7 copy-start.37
  1559.5 19.3 %copy-start.25 = (f32[2048]{0:T(1024)S(1)}, f32[2048]{0:T(1024)}, u32[]{:S(2)}) copy-start(f32[2048]{0:T(1024)} %copy-done.24) | copy-start | bytes 24580
  1559.5 165.9 %reduce-scatter.37.cloned.1.call-start = ((), (), s32[]{:S(2)}) async-start(), calls=%async_computation.19 | async-start | bytes 294912
  1578.7 164.3 %reduce-scatter.35.cloned.1.call-start = ((), (), s32[]{:S(2)}) async-start(), calls=%async_computation.18 | async-start | bytes 884736
  1589.6 168.8 %reduce-scatter.41.cloned.1.call-start = ((), (), s32[]{:S(2)}) async-start(), calls=%async_computation.21 | async-start | bytes 589824
  1622.9 149.9 %reduce-scatter.31.cloned.1.call-start = ((), (), s32[]{:S(2)}) async-start(), calls=%async_computation.16 | async-start | bytes 442368 | tf_op jit(solution)/shard_map/reduce_scatter | solution.py:103
  1700.3 6.7 copy-start.17
  (90 other events, 184.4 us)
Sparse Core Ops, SparseCore 0:
  15.9 47.6 all-gather.20
  65.9 36.9 all-gather.22
  105.1 51.9 all-gather.24
  159.3 51.6 all-gather.26
  1415.7 55.4 reduce-scatter.26
  1475.0 67.4 reduce-scatter.24
  1546.3 74.6 reduce-scatter.32
  1624.8 74.8 reduce-scatter.28
  1702.5 9.1 reduce-scatter.38
  1714.3 11.0 reduce-scatter.36
  1727.7 15.3 reduce-scatter.34
  1745.2 13.1 reduce-scatter.40
  1760.6 12.1 reduce-scatter.30
where the time goes:
time: 1790 us; the launch traced here: 1780 us
  matrix products  931 us (52%)
  other arithmetic  317 us (18%)
  local copies, waits for them, and re-layouts  200 us (11%)
  blocking collectives  155 us (9%)
  waiting for transfers between devices  152 us (8%)
  between operations  19.9 us (1%)
    dot_general x48, matrix products, forward_head(): jnp.dot(weights, values_in[:stop_row], preferred_element_type=jnp.float32)  156 us
    convert_element_type x48, other arithmetic, backward_head(): (probabilities * grad_weights - signed * row_inner).astype(jnp.bfloat16)  153 us
    dot_general x48, matrix products, backward_head(): jnp.einsum('qd,kd->qk', grad_block, values_in[:stop_row], preferred_eleme...  145 us
    dot_general x48, matrix products, backward_head(): jnp.einsum('qk,qd->kd', signed.astype(jnp.bfloat16), grad_block, preferre...  142 us
    unnamed x4, blocking collectives  128 us
    dot_general x48, matrix products, forward_head(): jnp.einsum('qd,kd->qk', queries[first_row:stop_row], keys_in[:stop_row],...  97.5 us
    while x168, local copies, waits for them, and re-layouts  77.3 us
    dot_general x48, matrix products, backward_head(): jnp.einsum('qd,kd->qk', query_block, keys_in[:stop_row], preferred_elemen...  74.3 us
  transfers between devices with their start and end apart: 13, of which 7 were waited for; matrix products, arithmetic and copies ran while one was open for 33% of the time, Pallas kernels for 0%

commit v1 on v0

v1 whole, which is shorter than its diff:
```python
import functools
import jax, jax.numpy as jnp
from jax import lax
from jax.experimental import pallas as pl
from jax.experimental.pallas import tpu as pltpu

HD = 64
LOG2E = 1.4426950408889634
LN2 = 0.6931471805599453
BIG = 3.0e38
NT = (((1,), (1,)), ((), ()))
NN = (((1,), (0,)), ((), ()))
TN = (((0,), (0,)), ((), ()))


def dot(a, b, dims):
    return lax.dot_general(a, b, dims, preferred_element_type=jnp.float32)


def split_lanes(x):
    lane = lax.broadcasted_iota(jnp.int32, x.shape, 1)
    zero = jnp.zeros_like(x)
    return jnp.where(lane < HD, x, zero), jnp.where(lane < HD, zero, x)


def attn_fwd_kernel(B, C, seq_ref, q_ref, k_ref, v_ref, o_ref, lse_ref, vt_ref, acc_ref):
    rows = q_ref.shape[0]
    nb = rows // B
    vt_ref[...] = v_ref[...].T
    per = seq_ref[0] // B

    def q_loop(qb, _):
        q0 = pl.multiple_of(qb * B, B)
        q2 = split_lanes(q_ref[pl.ds(q0, B), :] * jnp.asarray(HD ** -0.5, jnp.bfloat16))

        def block(k0, width, mask, state):
            kb = k_ref[pl.ds(k0, width), :]
            new = []
            for h in range(2):
                m, l, acc = state[h]
                s = dot(kb, q2[h], NT)
                t = jnp.minimum(jnp.maximum(s * BIG, -LOG2E), LOG2E)
                a = s * t
                if mask is not None:
                    a = jnp.where(mask, a, -1e30)
                m1 = jnp.max(a, axis=0, keepdims=True)
                if m is not None:
                    m1 = jnp.maximum(m, m1)
                e = jnp.exp2(a - m1)
                l1 = jnp.sum(e, axis=0, keepdims=True)
                w = (t * e).astype(jnp.bfloat16)
                pv = dot(vt_ref[h * HD:(h + 1) * HD, pl.ds(k0, width)], w, NN)
                if m is not None:
                    alpha = jnp.exp2(m - m1)
                    l1 = l1 + alpha * l
                    pv = pv + alpha * acc
                new.append((m1, l1, pv))
            return tuple(new)

        ki = lax.broadcasted_iota(jnp.int32, (B, B), 0)
        qi = lax.broadcasted_iota(jnp.int32, (B, B), 1)
        state = block(q0, B, ki <= qi, ((None,) * 3,) * 2)
        first = (qb // per) * per

        def k_loop(j, st):
            return block(pl.multiple_of((first + j) * B, B), B, None, st)

        state = lax.fori_loop(0, qb - first, k_loop, state)
        outs = []
        for h in range(2):
            m, l, acc = state[h]
            outs.append(acc * (1.0 / (l * LOG2E)))
            lse_ref[0, h:h + 1, pl.ds(q0, B)] = m + jnp.log2(l * LOG2E)
        o_ref[pl.ds(q0, B), :] = jnp.concatenate(outs, axis=0).T.astype(jnp.bfloat16)
        return 0

    lax.fori_loop(0, nb, q_loop, 0)


def attn_fwd(packed, seq, B=256, pairs=6):
    rows = packed.shape[0]
    width = packed.shape[1] // 3
    n = width // 128
    spec = lambda off: pl.BlockSpec((rows, 128), lambda p, s: (0, off + p))
    return pl.pallas_call(
        functools.partial(attn_fwd_kernel, B, 0),
        out_shape=(jax.ShapeDtypeStruct((rows, width), jnp.bfloat16),
                   jax.ShapeDtypeStruct((n, 2, rows), jnp.float32)),
        grid_spec=pltpu.PrefetchScalarGridSpec(
            num_scalar_prefetch=1, grid=(n,),
            in_specs=[spec(0), spec(n), spec(2 * n)],
            out_specs=(pl.BlockSpec((rows, 128), lambda p, s: (0, p)),
                       pl.BlockSpec((1, 2, rows), lambda p, s: (p, 0, 0))),
            scratch_shapes=[pltpu.VMEM((128, rows), jnp.bfloat16), pltpu.VMEM((128, B), jnp.float32)]),
        name="attn_fwd",
    )(seq, packed, packed, packed)


def attn_bwd_kernel(B, seq_ref, q_ref, k_ref, v_ref, g_ref, o_ref, lse_ref, gq_ref, gk_ref, gv_ref,
                    kt_ref, gqt_ref, gk_acc, gv_acc, del_ref):
    rows = q_ref.shape[0]
    nb = rows // B
    kt_ref[...] = k_ref[...].T
    per = seq_ref[0] // B
    prod = g_ref[...].astype(jnp.float32) * o_ref[...].astype(jnp.float32)
    r8 = lax.broadcasted_iota(jnp.int32, (8, 128), 0)
    c8 = lax.broadcasted_iota(jnp.int32, (8, 128), 1)
    sel = jnp.where(r8 == c8 // HD, LN2, 0.0).astype(jnp.float32)
    del_ref[...] = lax.dot_general(sel, prod, NT, precision=lax.Precision.HIGHEST,
                                   preferred_element_type=jnp.float32)
    gqt_ref[...] = jnp.zeros_like(gqt_ref)

    ki = lax.broadcasted_iota(jnp.int32, (B, B), 0)
    qi = lax.broadcasted_iota(jnp.int32, (B, B), 1)
    tri = ki <= qi
    scale = jnp.asarray(HD ** -0.5, jnp.bfloat16)

    def k_loop(kb, _):
        k0 = pl.multiple_of(kb * B, B)
        kblk = k_ref[pl.ds(k0, B), :]
        vblk = v_ref[pl.ds(k0, B), :]
        last = (kb // per + 1) * per
        gk_acc[...] = jnp.zeros_like(gk_acc)
        gv_acc[...] = jnp.zeros_like(gv_acc)

        def block(qb, mask):
            q0 = pl.multiple_of(qb * B, B)
            q2 = split_lanes(q_ref[pl.ds(q0, B), :] * scale)
            g2 = split_lanes(g_ref[pl.ds(q0, B), :])
            gk = None
            for h in range(2):
                s = dot(kblk, q2[h], NT)
                dw = dot(vblk, g2[h], NT)
                t = jnp.minimum(jnp.maximum(s * BIG, -LOG2E), LOG2E)
                lse = lse_ref[0, h:h + 1, pl.ds(q0, B)]
                dl = del_ref[h:h + 1, pl.ds(q0, B)]
                e = jnp.exp2(s * t - lse)
                if mask is not None:
                    e = jnp.where(mask, e, 0.0)
                w = (t * e).astype(jnp.bfloat16)
                ds = (e * (dw - t * dl)).astype(jnp.bfloat16)
                gv_acc[...] += dot(w, g2[h], NN)
                gk_acc[...] += dot(ds, q2[h], NN)
                gqt_ref[h * HD:(h + 1) * HD, pl.ds(q0, B)] += dot(
                    kt_ref[h * HD:(h + 1) * HD, pl.ds(k0, B)], ds, NN)

        block(kb, tri)

        def q_loop(qb, c):
            block(qb, None)
            return c

        lax.fori_loop(kb + 1, last, q_loop, 0)
        gk_ref[pl.ds(k0, B), :] = (gk_acc[...] * LOG2E).astype(jnp.bfloat16)
        gv_ref[pl.ds(k0, B), :] = gv_acc[...].astype(jnp.bfloat16)
        return 0

    lax.fori_loop(0, nb, k_loop, 0)
    gq_ref[...] = (gqt_ref[...] * (LOG2E * HD ** -0.5)).T.astype(jnp.bfloat16)


def attn_bwd(packed, grad_att, att, lse, seq, B=256):
    rows = packed.shape[0]
    width = packed.shape[1] // 3
    n = width // 128
    spec = lambda off: pl.BlockSpec((rows, 128), lambda p, s: (0, off + p))
    out = jax.ShapeDtypeStruct((rows, width), jnp.bfloat16)
    return pl.pallas_call(
        functools.partial(attn_bwd_kernel, B),
        out_shape=(out, out, out),
        grid_spec=pltpu.PrefetchScalarGridSpec(
            num_scalar_prefetch=1, grid=(n,),
            in_specs=[spec(0), spec(n), spec(2 * n), spec(0), spec(0),
                      pl.BlockSpec((1, 2, rows), lambda p, s: (p, 0, 0))],
            out_specs=(spec(0), spec(0), spec(0)),
            scratch_shapes=[pltpu.VMEM((128, rows), jnp.bfloat16), pltpu.VMEM((128, rows), jnp.float32),
                            pltpu.VMEM((B, 128), jnp.float32), pltpu.VMEM((B, 128), jnp.float32),
                            pltpu.VMEM((8, rows), jnp.float32)]),
        name="attn_bwd",
    )(seq, packed, packed, packed, grad_att, att, lse)


from jax.sharding import PartitionSpec as P

SHORT = 1024
LONG = 2048
EPS = 1e-05
BOTH = ("inner", "dp")
F32 = jnp.float32
BF16 = jnp.bfloat16


def mm(a, b, dims=NN):
    return lax.dot_general(a, b, dims, preferred_element_type=F32)


def normalise(values):
    center = values - jnp.mean(values, axis=-1, keepdims=True)
    rs = lax.rsqrt(jnp.mean(center * center, axis=-1, keepdims=True) + EPS)
    return center * rs, rs


def norm_back(grad, n, rs, gain):
    t = grad * gain
    back = rs * (t - jnp.mean(t, axis=-1, keepdims=True) - n * jnp.mean(t * n, axis=-1, keepdims=True))
    return back, jnp.sum(grad * n, axis=0), jnp.sum(grad, axis=0)


def gelu(u):
    return jax.nn.gelu(u, approximate=True)


def gather_weight(shard):
    rows, cols = shard.shape
    n_in, n_dp = lax.axis_size("inner"), lax.axis_size("dp")
    got = lax.all_gather(shard, BOTH, axis=0, tiled=True)
    return got.reshape(n_in, n_dp * rows, cols).transpose(1, 0, 2).reshape(n_dp * rows, n_in * cols)


def scatter_weight(grad):
    n_in = lax.axis_size("inner")
    rows, cols = grad.shape
    laid = grad.astype(BF16).reshape(rows, n_in, cols // n_in).transpose(1, 0, 2)
    laid = laid.reshape(n_in * rows, cols // n_in)
    return lax.psum_scatter(laid, BOTH, scatter_dimension=0, tiled=True).astype(F32)


def pack_rows(parts, tile):
    flat = jnp.concatenate(parts, axis=-1)
    fill = -flat.shape[-1] % tile
    return jnp.pad(flat, [(0, 0)] * (flat.ndim - 1) + [(0, fill)])


def gather_vectors(vectors):
    sizes = [v.shape[0] for v in vectors]
    mine = pack_rows(vectors, 2048).reshape(-1, 128)
    got = lax.all_gather(mine, ("dp", "inner"), axis=0, tiled=True)
    n = lax.axis_size("dp") * lax.axis_size("inner")
    got = got.reshape(n, -1)
    out, at = [], 0
    for size in sizes:
        out.append(got[:, at:at + size].reshape(-1).astype(F32))
        at += size
    return out


def scatter_vectors(vectors):
    n = lax.axis_size("dp") * lax.axis_size("inner")
    parts = [v.reshape(n, -1) for v in vectors]
    sizes = [p.shape[1] for p in parts]
    laid = pack_rows(parts, 1024).reshape(-1, 128)
    got = lax.psum_scatter(laid, ("dp", "inner"), scatter_dimension=0, tiled=True).reshape(-1)
    out, at = [], 0
    for size in sizes:
        out.append(got[at:at + size])
        at += size
    return out


def on_device(tokens, out_grad, norm1_gain, norm1_shift, qkv_weight, qkv_bias, proj_weight, proj_bias,
              norm2_gain, norm2_shift, up_weight, up_bias, down_weight, down_bias):
    n_dp = lax.axis_size("dp")
    seq = jnp.where(lax.axis_index("dp") < n_dp // 2, SHORT, LONG).astype(jnp.int32).reshape(1)
    gain1, shift1, b_qkv, b_proj, gain2, shift2, b_up, b_down = gather_vectors(
        [norm1_gain, norm1_shift, qkv_bias, proj_bias, norm2_gain, norm2_shift, up_bias, down_bias])
    w_qkv = gather_weight(qkv_weight)
    w_proj = gather_weight(proj_weight)
    w_up = gather_weight(up_weight)
    w_down = gather_weight(down_weight)

    x = tokens.astype(F32)
    n1, r1 = normalise(x)
    h1 = (n1 * gain1 + shift1).astype(BF16)
    packed = (mm(h1, w_qkv) + b_qkv).astype(BF16)
    attended, lse = attn_fwd(packed, seq)
    middle = x + mm(attended, w_proj) + b_proj
    n2, r2 = normalise(middle)
    h2 = (n2 * gain2 + shift2).astype(BF16)
    pre = mm(h2, w_up) + b_up
    active = gelu(pre).astype(BF16)
    output = (middle + mm(active, w_down) + b_down).astype(BF16)

    e = out_grad.astype(F32)
    g_down_bias = jnp.sum(e, axis=0)
    g_active = mm(out_grad, w_down, NT)
    _, pull = jax.vjp(gelu, pre)
    g_pre = pull(g_active)[0].astype(BF16)
    g_down = mm(active, out_grad, TN).astype(BF16)
    g_up = mm(h2, g_pre, TN).astype(BF16)
    g_up_bias = jnp.sum(g_pre.astype(F32), axis=0)
    g_h2 = mm(g_pre, w_up, NT)
    back2, g_gain2, g_shift2 = norm_back(g_h2, n2, r2, gain2)
    g_middle = e + back2
    g_z = g_middle.astype(BF16)
    g_proj_bias = jnp.sum(g_z.astype(F32), axis=0)
    g_proj = mm(attended, g_z, TN).astype(BF16)
    g_att = mm(g_z, w_proj, NT).astype(BF16)
    g_att, g_up, g_down, g_proj = lax.optimization_barrier((g_att, g_up, g_down, g_proj))
    s_down = scatter_weight(g_down)
    s_up = scatter_weight(g_up)
    s_proj = scatter_weight(g_proj)

    g_packed = jnp.concatenate(attn_bwd(packed, g_att, attended, lse, seq), axis=1)
    g_qkv = mm(h1, g_packed, TN).astype(BF16)
    g_qkv_bias = jnp.sum(g_packed.astype(F32), axis=0)
    s_qkv = scatter_weight(g_qkv)
    g_h1 = mm(g_packed, w_qkv, NT)
    back1, g_gain1, g_shift1 = norm_back(g_h1, n1, r1, gain1)
    grad_tokens = g_middle + back1
    v = scatter_vectors([g_gain1, g_shift1, g_qkv_bias, g_proj_bias, g_gain2, g_shift2, g_up_bias, g_down_bias])
    return (output, grad_tokens, v[0], v[1], s_qkv, v[2], s_proj, v[3], v[4], v[5], s_up, v[6], s_down, v[7])


def solution(mesh):
    rows = P(("dp", "inner"), None)
    vec = P(("dp", "inner"))
    mat = P("dp", "inner")
    params = (vec, vec, mat, vec, mat, vec) * 2
    return jax.shard_map(on_device, mesh=mesh, in_specs=(rows, rows) + params,
                         out_specs=(rows, rows) + params, check_vma=False)
```

time: 1790 us -> 1220 us (0.68)
  matrix products: 931 us -> 166 us
  waiting for transfers between devices: 152 us -> 620 us
  other arithmetic: 317 us -> 34.7 us
  Pallas kernels: 0 us -> 183 us
  blocking collectives: 155 us -> 70.4 us
  local copies, waits for them, and re-layouts: 200 us -> 118 us
    dot_general x348 -> x12, matrix products: 931 us -> 166 us  [mm(): return lax.dot_general(a, b, dims, preferred_element_type=F32)]
    reduce_scatter x5 -> x4, waiting for transfers between devices: 109 us -> 426 us  [scatter_weight(): lax.psum_scatter(laid, BOTH, scatter_dimension=0, tiled=True).astype(F32)]
    pallas_call x0 -> x2, Pallas kernels: none -> 183 us  [the longest x1 94.1 us: attn_fwd(): pl.pallas_call(functools.partial(attn_fwd_kernel, B, 0), out_shape=(jax.S...]
    convert_element_type x60 -> x7, other arithmetic: 159 us -> 7.12 us  [the longest x4 6.29 us: scatter_weight(): lax.psum_scatter(laid, BOTH, scatter_dimension=0, tiled=True).astype(F32)]
    unnamed x4 -> x0, blocking collectives: 128 us -> none
    unnamed x17 -> x10, waiting for transfers between devices: 42.3 us -> 156 us
    while x171 -> x0, local copies, waits for them, and re-layouts: 95 us -> none
    reduce_sum x58 -> x7, other arithmetic: 90.5 us -> 19.9 us  [the longest x2 11.1 us: norm_back(): return (back, jnp.sum(grad * n, axis=0), jnp.sum(grad, axis=0))]
  transfers between devices with their start and end apart: 13 -> 9, of which waited for: 7 -> 7; matrix products, arithmetic and copies ran while one was open for 33% -> 12% of each run, Pallas kernels for 0% -> 8%
where the time goes in v1:
time: 1220 us; the launch traced here: 1210 us
  waiting for transfers between devices  620 us (51%)
  Pallas kernels  183 us (15%)
  matrix products  166 us (14%)
  local copies, waits for them, and re-layouts  118 us (10%)
  blocking collectives  70.4 us (6%)
  other arithmetic  34.7 us (3%)
  between operations  14.9 us (1%)
    reduce_scatter x4, waiting for transfers between devices, scatter_weight(): lax.psum_scatter(laid, BOTH, scatter_dimension=0, tiled=True).astype(F32)  426 us
    dot_general x12, matrix products, mm(): return lax.dot_general(a, b, dims, preferred_element_type=F32)  166 us
    unnamed x10, waiting for transfers between devices  156 us
    pallas_call x1, Pallas kernels, attn_fwd(): pl.pallas_call(functools.partial(attn_fwd_kernel, B, 0), out_shape=(jax.S...  94.1 us
    pallas_call x1, Pallas kernels, attn_bwd(): pl.pallas_call(functools.partial(attn_bwd_kernel, B), out_shape=(out, out...  89.3 us
    all_gather x1, blocking collectives, gather_vectors(): got = lax.all_gather(mine, ('dp', 'inner'), axis=0, tiled=True)  70.4 us
    all_gather x4, waiting for transfers between devices, gather_weight(): got = lax.all_gather(shard, BOTH, axis=0, tiled=True)  38.7 us
    reshape x4, local copies, waits for them, and re-layouts, scatter_weight(): grad.astype(BF16).reshape(rows, n_in, cols // n_in).transpose(1, 0, 2)  33.4 us
  transfers between devices with their start and end apart: 9, of which 7 were waited for; matrix products, arithmetic and copies ran while one was open for 12% of the time, Pallas kernels for 8%

profile of v1, /device:TPU:0, one launch (start us, length us, event | category | flops | bytes accessed | tf_op | source)
XLA Modules:
  0.0 1208.6 jit_solution(6141811404564767902)
XLA Ops:
  10.1 3.2 copy.71
  13.5 70.4 %all_gather.15 = bf16[512,128]{1,0:T(8,128)(2,1)S(1)} all-gather(bf16[16,128]{1,0:T(8,128)(2,1)S(1)} %pad_bitcast_fusion), channel_id=1, replica_groups=mesh['dp'=16,'inner'=2] {'dp','inner'}, dimensions={0}, use_global_device_ids=true | all-gather | bytes 135168 | tf_op jit(solution)/shard_map/all_gather | solution.py:237
  85.4 4.7 copy.77
  91.5 2.4 copy.73
  93.9 35.8 %all-gather.5.cloned.1.call-done = bf16[1536,1152]{1,0:T(8,128)(2,1)} async-done(((bf16[48,1152]{1,0:T(8,128)(2,1)}), bf16[1536,1152]{1,0:T(8,128)(2,1)}) %all-gather.5.cloned.1.call-update) | async-done | bytes 3538960 | tf_op jit(solution)/shard_map/all_gather | solution.py:216
  129.7 5.8 copy.72
  135.5 12.7 %add_convert_fusion.q_ref.k_ref.v_ref = bf16[2048,2304]{1,0:T(8,128)(2,1)} fusion(bf16[768,2304]{0,1:T(8,128)(2,1)} %bitcast.65, f32[2304]{0:T(1024)S(1)} %reshape.250, bf16[2048,768]{0,1:T(8,128)(2,1)S(1)} %copy.71, f32[768]{0:T(1024)S(1)} %reshape.249, f32[768]{0:T(1024)S(1)} %reshape.248, f32[2048]{0:T(1024)S(1)} %add_rsqrt_fusion.1, ...), kind=kOutput, calls=%fused_computation.12 | convolution fusion | flops 7266631680 | bytes 16153600 | tf_op jit(solution)/shard_map/dot_general | solution.py:194
  148.2 94.1 %attn_fwd.1 = (bf16[2048,768]{1,0:T(8,128)(2,1)}, f32[6,2,2048]{2,1,0:T(2,128)}) custom-call(s32[1]{0:T(128)} %bitcast.seq_ref, bf16[2048,2304]{1,0:T(8,128)(2,1)} %add_convert_fusion.q_ref.k_ref.v_ref, bf16[2048,2304]{1,0:T(8,128)(2,1)} %add_convert_fusion.q_ref.k_ref.v_ref, bf16[2048,2304]{1,0:T(8,128)(2,1)} %add_convert_fusion.q_ref.k_ref.v_ref), custom_call_target="tpu_custom_call" | custom-call | tf_op jit(solution)/shard_map/attn_fwd/pallas_call | solution.py:85
  242.3 4.9 fusion.28
  247.2 2.6 copy-done.2
  250.6 6.7 copy.74
  257.3 2.8 all-gather.11.cloned.1.call-done
  260.2 6.6 copy.75
  266.8 27.2 %multiply_convert_fusion = (bf16[2048,3072]{1,0:T(8,128)(2,1)}, f32[2048,3072]{1,0:T(8,128)}) fusion(f32[3072]{0:T(1024)S(1)} %reshape.254, bf16[768,3072]{0,1:T(8,128)(2,1)} %bitcast.61, f32[2048,768]{0,1:T(8,128)} %copy-done.2, f32[768]{0:T(1024)S(1)} %reshape.253, f32[768]{0:T(1024)S(1)} %reshape.252, f32[2048]{0:T(1024)S(1)} %add_rsqrt_fusion, ...), kind=kOutput, calls=%fused_computation.10 | convolution fusion | flops 9734455296 | bytes 48793600 | tf_op jit(solution)/shard_map/dot_general | solution.py:194
  294.0 33.1 %convert_reduce_fusion = (f32[3072]{0:T(1024)S(1)}, bf16[2048,3072]{1,0:T(8,128)(2,1)}) fusion(f32[2048,3072]{1,0:T(8,128)} %get-tuple-element.112, f32[3072]{0:T(1024)S(1)} %reshape.254, bf16[2048,768]{1,0:T(8,128)(2,1)} %param.15, bf16[3072,768]{0,1:T(8,128)(2,1)} %bitcast.57), kind=kOutput, calls=%fused_computation.9 | convolution fusion | flops 9808376832 | bytes 45637632 | tf_op jit(solution)/shard_map/dot_general | solution.py:194
  327.1 16.6 %fusion.30 = (f32[768]{0:T(1024)S(1)}, f32[2048,768]{1,0:T(8,128)}) fusion(bf16[2048,3072]{1,0:T(8,128)(2,1)} %get-tuple-element.118, bf16[768,3072]{0,1:T(8,128)(2,1)} %bitcast.62), kind=kOutput, calls=%fused_computation.74 | convolution fusion | flops 9665248256 | bytes 23596032 | tf_op jit(solution)/shard_map/dot_general | solution.py:194
  343.8 11.9 convolution_convert_fusion.1
  355.6 6.7 copy.78
  362.4 6.6 multiply_reduce_fusion
  370.1 5.4 convert_reduce_fusion.4
  375.5 3.7 convolution_convert_fusion.4
  379.3 4.1 convolution_convert_fusion.3.g_ref
  385.4 12.3 %convolution_convert_fusion = bf16[3072,768]{1,0:T(8,128)(2,1)} fusion(bf16[2048,3072]{1,0:T(8,128)(2,1)S(1)} %bitcast.72, bf16[2048,768]{1,0:T(8,128)(2,1)S(1)} %copy-done.7), kind=kOutput, calls=%fused_computation.42 | convolution fusion | flops 9666035712 | bytes 20447232 | tf_op jit(solution)/shard_map/dot_general | solution.py:194
  397.7 89.3 %attn_bwd.1 = (bf16[2048,768]{1,0:T(8,128)(2,1)}, bf16[2048,768]{1,0:T(8,128)(2,1)}, bf16[2048,768]{1,0:T(8,128)(2,1)}) custom-call(s32[1]{0:T(128)} %bitcast.seq_ref, bf16[2048,2304]{1,0:T(8,128)(2,1)} %add_convert_fusion.q_ref.k_ref.v_ref, bf16[2048,2304]{1,0:T(8,128)(2,1)} %add_convert_fusion.q_ref.k_ref.v_ref, ...), custom_call_target="tpu_custom_call" | custom-call | tf_op jit(solution)/shard_map/attn_bwd/pallas_call | solution.py:168
  487.1 2.2 constant_dynamic-update-slice_fusion.2
  492.1 9.6 fusion.29
  503.1 6.7 copy.79
  509.8 4.5 fusion.19
  515.9 3.6 reshape.242
  519.5 2.5 copy.83
  522.1 13.1 %convolution_convert_fusion.2 = bf16[768,2304]{1,0:T(8,128)(2,1)} fusion(bf16[2048,2304]{1,0:T(8,128)(2,1)} %copy-done.5, bf16[2048,768]{0,1:T(8,128)(2,1)S(1)} %copy-done.1, f32[768]{0:T(1024)S(1)} %copy-done.20, f32[768]{0:T(1024)S(1)} %copy-done.18, f32[2048]{0:T(1024)S(1)} %copy-done.15, f32[2048]{0:T(1024)S(1)} %copy-done.13), kind=kOutput, calls=%fused_computation.44 | convolution fusion | flops 7258963968 | bytes 16144384 | tf_op jit(solution)/shard_map/dot_general | solution.py:194
  535.2 7.8 reshape.240
  543.1 4.2 copy.82
  547.4 11.9 reshape.244
  559.3 5.2 copy.84
  564.5 10.1 reshape.246
  574.6 5.1 copy.85
  579.9 7.6 fusion.18
  587.5 6.6 copy.87
  594.1 17.0 %add_convert_fusion.1 = bf16[2048,768]{0,1:T(8,128)(2,1)S(1)} fusion(f32[2048,768]{0,1:T(8,128)} %copy-done.2, bf16[2048,3072]{1,0:T(8,128)(2,1)} %get-tuple-element.111, bf16[3072,768]{0,1:T(8,128)(2,1)} %bitcast.58, f32[768]{0:T(1024)S(1)} %reshape.255), kind=kOutput, calls=%fused_computation.36 | convolution fusion | flops 9668395008 | bytes 26741760 | tf_op jit(solution)/shard_map/dot_general | solution.py:194
  611.1 2.8 copy.86
  613.9 153.2 %all-reduce.5.cloned.1.call-done = f32[256,128]{1,0:T(8,128)} async-done(((f32[256,128]{1,0:T(8,128)}), f32[256,128]{1,0:T(8,128)}) %all-reduce.5.cloned.1.call-update) | async-done | bytes 131088
  769.5 98.4 %reduce-scatter.7.cloned.1.call-done = bf16[48,384]{1,0:T(8,128)(2,1)} async-done(((bf16[1536,384]{1,0:T(8,128)(2,1)}), bf16[48,384]{1,0:T(8,128)(2,1)}) %reduce-scatter.7.cloned.1.call-update) | async-done | bytes 36880 | tf_op jit(solution)/shard_map/reduce_scatter | solution.py:225
  869.3 106.6 %reduce-scatter.5.cloned.1.call-done = bf16[48,1152]{1,0:T(8,128)(2,1)} async-done(((bf16[1536,1152]{1,0:T(8,128)(2,1)}), bf16[48,1152]{1,0:T(8,128)(2,1)}) %reduce-scatter.5.cloned.1.call-update) | async-done | bytes 110608 | tf_op jit(solution)/shard_map/reduce_scatter | solution.py:225
  977.5 110.4 %reduce-scatter.9.cloned.1.call-done = bf16[48,1536]{1,0:T(8,128)(2,1)} async-done(((bf16[1536,1536]{1,0:T(8,128)(2,1)}), bf16[48,1536]{1,0:T(8,128)(2,1)}) %reduce-scatter.9.cloned.1.call-update) | async-done | bytes 147472 | tf_op jit(solution)/shard_map/reduce_scatter | solution.py:225
  1088.0 1.6 convert_element_type.182
  1089.6 110.4 %reduce-scatter.11.cloned.1.call-done = bf16[192,384]{1,0:T(8,128)(2,1)} async-done(((bf16[6144,384]{1,0:T(8,128)(2,1)}), bf16[192,384]{1,0:T(8,128)(2,1)}) %reduce-scatter.11.cloned.1.call-update) | async-done | bytes 147472 | tf_op jit(solution)/shard_map/reduce_scatter | solution.py:225
  1200.0 1.6 convert_element_type.183
  (140 shorter events, 21.1 us)
Async XLA Ops:
  7.2 6.1 copy-start.21
  7.2 6.1 copy-start.22
  7.2 6.1 copy-start.23
  7.2 6.1 copy-start.24
  7.2 6.1 copy-start.25
  7.2 6.1 copy-start.26
  7.2 6.1 copy-start.27
  7.3 6.1 copy-start.28
  7.3 84.3 %all-gather.7.cloned.1.call-start = ((), (), s32[]{:S(2)}) async-start(), calls=%async_computation.5 | async-start | bytes 1216512 | tf_op jit(solution)/shard_map/all_gather | solution.py:216
  8.0 121.7 %all-gather.5.cloned.1.call-start = ((), (), s32[]{:S(2)}) async-start(), calls=%async_computation.4 | async-start | bytes 3649536 | tf_op jit(solution)/shard_map/all_gather | solution.py:216
  8.7 241.8 %all-gather.9.cloned.1.call-start = ((), (), s32[]{:S(2)}) async-start(), calls=%async_computation.6 | async-start | bytes 4866048 | tf_op jit(solution)/shard_map/all_gather | solution.py:216
  9.5 250.7 %all-gather.11.cloned.1.call-start = ((), (), s32[]{:S(2)}) async-start(), calls=%async_computation.7 | async-start | bytes 4866048 | tf_op jit(solution)/shard_map/all_gather | solution.py:216
  10.1 757.0 %all-reduce.5.cloned.1.call-start = ((), (), s32[]{:S(2)}) async-start(), calls=%async_computation.12 | async-start | bytes 262144
  13.4 228.9 %copy-start = (bf16[2048,768]{0,1:T(8,128)(2,1)}, bf16[2048,768]{0,1:T(8,128)(2,1)S(1)}, u32[]{:S(2)}) copy-start(bf16[2048,768]{0,1:T(8,128)(2,1)S(1)} %copy.71) | copy-start | bytes 9437188
  84.7 50.7 %copy-start.17 = (f32[768]{0:T(1024)}, f32[768]{0:T(1024)S(1)}, u32[]{:S(2)}) copy-start(f32[768]{0:T(1024)S(1)} %reshape.248) | copy-start | bytes 9220
  84.8 50.6 %copy-start.19 = (f32[768]{0:T(1024)}, f32[768]{0:T(1024)S(1)}, u32[]{:S(2)}) copy-start(f32[768]{0:T(1024)S(1)} %reshape.249) | copy-start | bytes 9220
  90.6 44.9 %copy-start.12 = (f32[2048]{0:T(1024)}, f32[2048]{0:T(1024)S(1)}, u32[]{:S(2)}) copy-start(f32[2048]{0:T(1024)S(1)} %broadcast_multiply_fusion.5) | copy-start | bytes 24580
  91.5 56.7 %copy-start.14 = (f32[2048]{0:T(1024)}, f32[2048]{0:T(1024)S(1)}, u32[]{:S(2)}) copy-start(f32[2048]{0:T(1024)S(1)} %add_rsqrt_fusion.1) | copy-start | bytes 24580
  247.2 2.6 copy-start.2
  266.8 76.9 %slice-start = ((s8[6291456]{0:T(1024)(128)(4,1)}), s8[2097152]{0:T(1024)(128)(4,1)S(1)}, s32[]{:S(2)}) async-start(s8[6291456]{0:T(1024)(128)(4,1)} %bitcast.47), calls=%async_computation.13 | async-start | bytes 4194304
  294.0 49.7 %slice-start.1 = ((s8[6291456]{0:T(1024)(128)(4,1)}), s8[4194304]{0:T(1024)(128)(4,1)S(1)}, s32[]{:S(2)}) async-start(s8[6291456]{0:T(1024)(128)(4,1)} %bitcast.47), calls=%async_computation.14 | async-start | bytes 8388608
  327.1 16.6 %copy-start.29 = (bf16[2048,3072]{1,0:T(8,128)(2,1)S(1)}, bf16[2048,3072]{1,0:T(8,128)(2,1)}, u32[]{:S(2)}) copy-start(bf16[2048,3072]{1,0:T(8,128)(2,1)} %get-tuple-element.118) | copy-start | bytes 37748740
  355.6 13.3 %slice-start.2 = ((s8[6291456]{0:T(1024)(128)(4,1)}), s8[2097152]{0:T(1024)(128)(4,1)S(1)}, s32[]{:S(2)}) async-start(s8[6291456]{0:T(1024)(128)(4,1)} %bitcast.49), calls=%async_computation.15 | async-start | bytes 4194304
  362.4 6.6 slice-start.3
  362.4 7.7 copy-start.3
  370.1 5.4 copy-start.10
  375.5 3.8 copy-start.4
  375.5 3.8 copy-start.11
  375.5 7.9 slice-start.4
  375.5 7.9 slice-start.5
  379.3 4.9 copy-start.7
  379.3 6.1 slice-start.6
  487.1 2.8 copy-start.9
  487.1 3.8 copy-start.8
  489.9 2.2 copy-start.6
  492.1 9.6 copy-start.5
  503.1 6.7 copy-start.1
  503.1 6.7 copy-start.13
  503.1 6.7 copy-start.15
  503.1 6.7 copy-start.18
  509.8 12.3 %copy-start.20 = (f32[768]{0:T(1024)S(1)}, f32[768]{0:T(1024)}, u32[]{:S(2)}) copy-start(f32[768]{0:T(1024)} %copy-done.19) | copy-start | bytes 9220
  515.9 352.0 %reduce-scatter.7.cloned.1.call-start = ((), (), s32[]{:S(2)}) async-start(), calls=%async_computation.9 | async-start | bytes 1216512 | tf_op jit(solution)/shard_map/reduce_scatter | solution.py:225
  522.1 453.9 %reduce-scatter.5.cloned.1.call-start = ((), (), s32[]{:S(2)}) async-start(), calls=%async_computation.8 | async-start | bytes 3649536 | tf_op jit(solution)/shard_map/reduce_scatter | solution.py:225
  547.3 540.7 %reduce-scatter.9.cloned.1.call-start = ((), (), s32[]{:S(2)}) async-start(), calls=%async_computation.10 | async-start | bytes 4866048 | tf_op jit(solution)/shard_map/reduce_scatter | solution.py:225
  564.5 635.5 %reduce-scatter.11.cloned.1.call-start = ((), (), s32[]{:S(2)}) async-start(), calls=%async_computation.11 | async-start | bytes 4866048 | tf_op jit(solution)/shard_map/reduce_scatter | solution.py:225
  574.6 5.2 copy-start.16
Sparse Core Ops, SparseCore 0:
  11.0 56.8 all-gather.6
  70.8 58.8 all-gather.4
  132.6 62.5 all-gather.8
  197.9 62.1 all-gather.10
  516.0 251.0 all-reduce.4
  772.0 95.8 reduce-scatter.6
  873.3 102.5 reduce-scatter.4
  981.4 106.5 reduce-scatter.8
  1093.5 106.4 reduce-scatter.10

commit v2 on v1

--- a/solution.py
+++ b/solution.py
@@ -23,7 +23,7 @@
     return jnp.where(lane < HD, x, zero), jnp.where(lane < HD, zero, x)
 
 
-def attn_fwd_kernel(B, C, seq_ref, q_ref, k_ref, v_ref, o_ref, lse_ref, vt_ref, acc_ref):
+def attn_fwd_kernel(B, seq_ref, q_ref, k_ref, v_ref, o_ref, lse_ref, vt_ref, acc_ref):
     rows = q_ref.shape[0]
     nb = rows // B
     vt_ref[...] = v_ref[...].T
@@ -77,13 +77,13 @@
     lax.fori_loop(0, nb, q_loop, 0)
 
 
-def attn_fwd(packed, seq, B=256, pairs=6):
+def attn_fwd(packed, seq, B=512):
     rows = packed.shape[0]
     width = packed.shape[1] // 3
     n = width // 128
     spec = lambda off: pl.BlockSpec((rows, 128), lambda p, s: (0, off + p))
     return pl.pallas_call(
-        functools.partial(attn_fwd_kernel, B, 0),
+        functools.partial(attn_fwd_kernel, B),
         out_shape=(jax.ShapeDtypeStruct((rows, width), jnp.bfloat16),
                    jax.ShapeDtypeStruct((n, 2, rows), jnp.float32)),
         grid_spec=pltpu.PrefetchScalarGridSpec(
@@ -127,7 +127,6 @@
             q0 = pl.multiple_of(qb * B, B)
             q2 = split_lanes(q_ref[pl.ds(q0, B), :] * scale)
             g2 = split_lanes(g_ref[pl.ds(q0, B), :])
-            gk = None
             for h in range(2):
                 s = dot(kblk, q2[h], NT)
                 dw = dot(vblk, g2[h], NT)
@@ -159,7 +158,7 @@
     gq_ref[...] = (gqt_ref[...] * (LOG2E * HD ** -0.5)).T.astype(jnp.bfloat16)
 
 
-def attn_bwd(packed, grad_att, att, lse, seq, B=256):
+def attn_bwd(packed, grad_att, att, lse, seq, B=512):
     rows = packed.shape[0]
     width = packed.shape[1] // 3
     n = width // 128
@@ -182,6 +181,7 @@
 
 from jax.sharding import PartitionSpec as P
 
+
 SHORT = 1024
 LONG = 2048
 EPS = 1e-05
@@ -210,63 +210,89 @@
     return jax.nn.gelu(u, approximate=True)
 
 
-def gather_weight(shard):
-    rows, cols = shard.shape
+def lay_vectors(parts, width):
+    flat = jnp.concatenate(parts, axis=1).astype(BF16)
+    fill = -flat.shape[1] % (16 * width)
+    return jnp.pad(flat, ((0, 0), (0, fill))).reshape(flat.shape[0], -1, width)
+
+
+def gather_all(weights, vectors, width):
     n_in, n_dp = lax.axis_size("inner"), lax.axis_size("dp")
-    got = lax.all_gather(shard, BOTH, axis=0, tiled=True)
-    return got.reshape(n_in, n_dp * rows, cols).transpose(1, 0, 2).reshape(n_dp * rows, n_in * cols)
-
-
-def scatter_weight(grad):
-    n_in = lax.axis_size("inner")
-    rows, cols = grad.shape
-    laid = grad.astype(BF16).reshape(rows, n_in, cols // n_in).transpose(1, 0, 2)
-    laid = laid.reshape(n_in * rows, cols // n_in)
-    return lax.psum_scatter(laid, BOTH, scatter_dimension=0, tiled=True).astype(F32)
-
-
-def pack_rows(parts, tile):
-    flat = jnp.concatenate(parts, axis=-1)
-    fill = -flat.shape[-1] % tile
-    return jnp.pad(flat, [(0, 0)] * (flat.ndim - 1) + [(0, fill)])
-
-
-def gather_vectors(vectors):
-    sizes = [v.shape[0] for v in vectors]
-    mine = pack_rows(vectors, 2048).reshape(-1, 128)
-    got = lax.all_gather(mine, ("dp", "inner"), axis=0, tiled=True)
-    n = lax.axis_size("dp") * lax.axis_size("inner")
-    got = got.reshape(n, -1)
+    pieces, plan = [], []
+    for w in weights:
+        count = w.shape[1] // width
+        plan.append((w.shape[0], count))
+        pieces += [w[:, j * width:(j + 1) * width] for j in range(count)]
+    if vectors:
+        pieces.append(lay_vectors([v.reshape(1, -1) for v in vectors], width)[0])
+    mine = jnp.concatenate(pieces, axis=0)
+    got = lax.all_gather(mine, BOTH, axis=0, tiled=True).reshape(n_in, n_dp, mine.shape[0], width)
+    whole, at = [], 0
+    for rows, count in plan:
+        cols = []
+        for i in range(n_in):
+            for j in range(count):
+                lo = at + j * rows
+                cols.append(got[i, :, lo:lo + rows].reshape(n_dp * rows, width))
+        whole.append(jnp.concatenate(cols, axis=1))
+        at += rows * count
+    if not vectors:
+        return whole, []
+    flat = got[:, :, at:].transpose(1, 0, 2, 3).reshape(n_dp * n_in, -1)
+    vecs, at = [], 0
+    for v in vectors:
+        vecs.append(flat[:, at:at + v.shape[0]].reshape(-1).astype(F32))
+        at += v.shape[0]
+    return whole, vecs
+
+
+def lay_grads(grads, vectors, width):
+    n_in, n_dp = lax.axis_size("inner"), lax.axis_size("dp")
+    if vectors:
+        vecs = lay_vectors([v.reshape(n_dp * n_in, -1) for v in vectors], width)
+        vecs = vecs.reshape(n_dp, n_in, -1, width)
+    halves = []
+    for i in range(n_in):
+        pieces = []
+        for g in grads:
+            part = g.shape[1] // n_in
+            for j in range(part // width):
+                lo = i * part + j * width
+                pieces.append(g[:, lo:lo + width].reshape(n_dp, -1, width))
+        if vectors:
+            pieces.append(vecs[:, i])
+        halves.append(jnp.concatenate(pieces, axis=1))
+    laid = jnp.concatenate(halves, axis=0)
+    return laid.reshape(-1, width)
+
+
+def take_grads(mine, shapes, sizes, width):
     out, at = [], 0
+    for rows, cols in shapes:
+        count = cols // width
+        out.append(jnp.concatenate([mine[at + j * rows:at + (j + 1) * rows] for j in range(count)], axis=1))
+        at += rows * count
+    flat = mine[at:].reshape(-1)
+    vecs, at = [], 0
     for size in sizes:
-        out.append(got[:, at:at + size].reshape(-1).astype(F32))
+        vecs.append(flat[at:at + size])
         at += size
-    return out
-
-
-def scatter_vectors(vectors):
-    n = lax.axis_size("dp") * lax.axis_size("inner")
-    parts = [v.reshape(n, -1) for v in vectors]
-    sizes = [p.shape[1] for p in parts]
-    laid = pack_rows(parts, 1024).reshape(-1, 128)
-    got = lax.psum_scatter(laid, ("dp", "inner"), scatter_dimension=0, tiled=True).reshape(-1)
-    out, at = [], 0
-    for size in sizes:
-        out.append(got[at:at + size])
-        at += size
-    return out
+    return [o.astype(F32) for o in out], [v.astype(F32) for v in vecs]
+
+
+def scatter(laid):
+    return lax.psum_scatter(laid, BOTH, scatter_dimension=0, tiled=True)
 
 
 def on_device(tokens, out_grad, norm1_gain, norm1_shift, qkv_weight, qkv_bias, proj_weight, proj_bias,
               norm2_gain, norm2_shift, up_weight, up_bias, down_weight, down_bias):
     n_dp = lax.axis_size("dp")
     seq = jnp.where(lax.axis_index("dp") < n_dp // 2, SHORT, LONG).astype(jnp.int32).reshape(1)
-    gain1, shift1, b_qkv, b_proj, gain2, shift2, b_up, b_down = gather_vectors(
-        [norm1_gain, norm1_shift, qkv_bias, proj_bias, norm2_gain, norm2_shift, up_bias, down_bias])
-    w_qkv = gather_weight(qkv_weight)
-    w_proj = gather_weight(proj_weight)
-    w_up = gather_weight(up_weight)
-    w_down = gather_weight(down_weight)
+    width = proj_weight.shape[1]
+    vectors = [norm1_gain, norm1_shift, qkv_bias, proj_bias, norm2_gain, norm2_shift, up_bias, down_bias]
+    (w_qkv,), vecs = gather_all([qkv_weight], vectors, width)
+    gain1, shift1, b_qkv, b_proj, gain2, shift2, b_up, b_down = vecs
+    (w_proj, w_up, w_down), _ = gather_all([proj_weight, up_weight, down_weight], [], width)
 
     x = tokens.astype(F32)
     n1, r1 = normalise(x)
@@ -295,19 +321,22 @@
     g_proj_bias = jnp.sum(g_z.astype(F32), axis=0)
     g_proj = mm(attended, g_z, TN).astype(BF16)
     g_att = mm(g_z, w_proj, NT).astype(BF16)
-    g_att, g_up, g_down, g_proj = lax.optimization_barrier((g_att, g_up, g_down, g_proj))
-    s_down = scatter_weight(g_down)
-    s_up = scatter_weight(g_up)
-    s_proj = scatter_weight(g_proj)
+    laid = lay_grads([g_proj, g_up, g_down], [], width)
+    g_att, laid = lax.optimization_barrier((g_att, laid))
+    mine = scatter(laid)
+    (s_proj, s_up, s_down), _ = take_grads(
+        mine, [proj_weight.shape, up_weight.shape, down_weight.shape], [], width)
 
     g_packed = jnp.concatenate(attn_bwd(packed, g_att, attended, lse, seq), axis=1)
     g_qkv = mm(h1, g_packed, TN).astype(BF16)
     g_qkv_bias = jnp.sum(g_packed.astype(F32), axis=0)
-    s_qkv = scatter_weight(g_qkv)
     g_h1 = mm(g_packed, w_qkv, NT)
     back1, g_gain1, g_shift1 = norm_back(g_h1, n1, r1, gain1)
     grad_tokens = g_middle + back1
-    v = scatter_vectors([g_gain1, g_shift1, g_qkv_bias, g_proj_bias, g_gain2, g_shift2, g_up_bias, g_down_bias])
+    g_vecs = [g_gain1, g_shift1, g_qkv_bias, g_proj_bias, g_gain2, g_shift2, g_up_bias, g_down_bias]
+    laid = lay_grads([g_qkv], g_vecs, width)
+    mine = scatter(laid)
+    (s_qkv,), v = take_grads(mine, [qkv_weight.shape], [u.shape[0] for u in vectors], width)
     return (output, grad_tokens, v[0], v[1], s_qkv, v[2], s_proj, v[3], v[4], v[5], s_up, v[6], s_down, v[7])
 
 
@@ -316,5 +345,6 @@
     vec = P(("dp", "inner"))
     mat = P("dp", "inner")
     params = (vec, vec, mat, vec, mat, vec) * 2
+
     return jax.shard_map(on_device, mesh=mesh, in_specs=(rows, rows) + params,
                          out_specs=(rows, rows) + params, check_vma=False)

time: 1220 us -> 774 us (0.63)
  waiting for transfers between devices: 620 us -> 332 us
  blocking collectives: 70.4 us -> 0 us
  Pallas kernels: 183 us -> 119 us
  local copies, waits for them, and re-layouts: 118 us -> 87.6 us
  other arithmetic: 34.7 us -> 49.9 us
    unnamed x10 -> x4, waiting for transfers between devices: 156 us -> 0.57 us
    reduce_scatter x4 -> x2, waiting for transfers between devices: 426 us -> 271 us  [scatter(): return lax.psum_scatter(laid, BOTH, scatter_dimension=0, tiled=True)]
    all_gather x1 -> x0, blocking collectives: 70.4 us -> none  [gather_vectors(): got = lax.all_gather(mine, ('dp', 'inner'), axis=0, tiled=True)]
    pallas_call x1, Pallas kernels: 94.1 us -> 49.1 us  [attn_fwd(): pl.pallas_call(functools.partial(attn_fwd_kernel, B), out_shape=(jax.Shap...]
    transpose x8 -> x0, local copies, waits for them, and re-layouts: 38.6 us -> none  [the longest x4 21.5 us: gather_weight(): got.reshape(n_in, n_dp * rows, cols).transpose(1, 0, 2)]
    reshape x16 -> x9, local copies, waits for them, and re-layouts: 35.4 us -> 1.36 us  [the longest x8 1.35 us: lay_grads(): vecs = lay_vectors([v.reshape(n_dp * n_in, -1) for v in vectors], width)]
    all_gather x4 -> x2, waiting for transfers between devices: 38.7 us -> 60.2 us  [gather_all(): lax.all_gather(mine, BOTH, axis=0, tiled=True)]
    pallas_call x1, Pallas kernels: 89.3 us -> 69.8 us  [attn_bwd(): pl.pallas_call(functools.partial(attn_bwd_kernel, B), out_shape=(out, out...]
  transfers between devices with their start and end apart: 9 -> 4, of which waited for: 7 -> 4; matrix products, arithmetic and copies ran while one was open for 12% -> 11% of each run, Pallas kernels for 8% -> 6%
where the time goes in v2:
time: 774 us; the launch traced here: 765 us
  waiting for transfers between devices  332 us (43%)
  matrix products  162 us (21%)
  Pallas kernels  119 us (15%)
  local copies, waits for them, and re-layouts  87.6 us (11%)
  other arithmetic  49.9 us (6%)
  between operations  14.7 us (2%)
    reduce_scatter x2, waiting for transfers between devices, scatter(): return lax.psum_scatter(laid, BOTH, scatter_dimension=0, tiled=True)  271 us
    dot_general x12, matrix products, mm(): return lax.dot_general(a, b, dims, preferred_element_type=F32)  162 us
    pallas_call x1, Pallas kernels, attn_bwd(): pl.pallas_call(functools.partial(attn_bwd_kernel, B), out_shape=(out, out...  69.8 us
    all_gather x2, waiting for transfers between devices, gather_all(): lax.all_gather(mine, BOTH, axis=0, tiled=True)  60.2 us
    pallas_call x1, Pallas kernels, attn_fwd(): pl.pallas_call(functools.partial(attn_fwd_kernel, B), out_shape=(jax.Shap...  49.1 us
    unnamed x116, local copies, waits for them, and re-layouts  41.6 us
  transfers between devices with their start and end apart: 4, of which 4 were waited for; matrix products, arithmetic and copies ran while one was open for 11% of the time, Pallas kernels for 6%

profile of v2, /device:TPU:0, one launch (start us, length us, event | category | flops | bytes accessed | tf_op | source)
XLA Modules:
  0.0 765.4 jit_solution(9404367483145806576)
XLA Ops:
  15.3 3.2 copy.37
  18.6 5.5 copy.40
  24.1 2.4 reduce.3
  28.5 46.6 %all-gather.3.cloned.1.call-done = bf16[5120,384]{1,0:T(8,128)(2,1)} async-done(((bf16[160,384]{1,0:T(8,128)(2,1)}), bf16[5120,384]{1,0:T(8,128)(2,1)}) %all-gather.3.cloned.1.call-update) | async-done | bytes 3932176 | tf_op jit(solution)/shard_map/all_gather | solution.py:229
  77.0 1.4 reshape.304
  78.4 1.4 reshape.305
  80.5 1.4 reshape.306
  81.9 1.4 reshape.307
  83.3 1.4 reshape.308
  84.7 1.4 reshape.309
  87.5 2.3 fusion.38
  90.5 11.1 %add_convert_fusion.q_ref.k_ref.v_ref = bf16[2048,2304]{1,0:T(8,128)(2,1)} fusion(bf16[768,2304]{1,0:T(8,128)(2,1)S(1)} %constant_dynamic-update-slice_fusion, f32[2304]{0:T(1024)S(1)} %copy-done.27, bf16[2048,768]{0,1:T(8,128)(2,1)S(1)} %copy.37, f32[768]{0:T(1024)S(1)} %copy-done.29, f32[768]{0:T(1024)S(1)} %copy-done.23, f32[2048]{0:T(1024)S(1)} %add_rsqrt_fusion.1, ...), kind=kOutput, calls=%fused_computation.15 | convolution fusion | flops 7266631680 | bytes 16153600 | tf_op jit(solution)/shard_map/dot_general | solution.py:194
  101.7 49.1 %attn_fwd.1 = (bf16[2048,768]{1,0:T(8,128)(2,1)}, f32[6,2,2048]{2,1,0:T(2,128)}) custom-call(s32[1]{0:T(128)} %bitcast.seq_ref, bf16[2048,2304]{1,0:T(8,128)(2,1)} %add_convert_fusion.q_ref.k_ref.v_ref, bf16[2048,2304]{1,0:T(8,128)(2,1)} %add_convert_fusion.q_ref.k_ref.v_ref, bf16[2048,2304]{1,0:T(8,128)(2,1)} %add_convert_fusion.q_ref.k_ref.v_ref), custom_call_target="tpu_custom_call" | custom-call | tf_op jit(solution)/shard_map/attn_fwd/pallas_call | solution.py:85
  150.8 13.6 %all-gather.5.cloned.1.call-done = bf16[13824,384]{1,0:T(8,128)(2,1)} async-done(((bf16[432,384]{1,0:T(8,128)(2,1)}), bf16[13824,384]{1,0:T(8,128)(2,1)}) %all-gather.5.cloned.1.call-update) | async-done | bytes 10616848 | tf_op jit(solution)/shard_map/all_gather | solution.py:229
  164.4 3.3 fusion.35
  167.8 5.5 fusion.34
  173.3 3.2 fusion.44
  178.3 1.4 constant_dynamic-update-slice_fusion.18
  185.3 27.1 %multiply_convert_fusion = (bf16[2048,3072]{1,0:T(8,128)(2,1)}, f32[2048,3072]{1,0:T(8,128)}) fusion(f32[3072]{0:T(1024)S(1)} %reshape.310, bf16[768,3072]{1,0:T(8,128)(2,1)} %constant_dynamic-update-slice_fusion.12, f32[2048,768]{0,1:T(8,128)} %copy-done.2, f32[768]{0:T(1024)S(1)} %copy-done.31, f32[768]{0:T(1024)S(1)} %copy-done.25, ...), kind=kOutput, calls=%fused_computation.14 | convolution fusion | flops 9734455296 | bytes 48793600 | tf_op jit(solution)/shard_map/dot_general | solution.py:194
  212.4 33.9 %fusion.47 = (bf16[3072]{0:T(1024)(128)(2,1)}, bf16[2048,3072]{1,0:T(8,128)(2,1)}) fusion(f32[2048,3072]{1,0:T(8,128)} %get-tuple-element.128, f32[3072]{0:T(1024)S(1)} %reshape.310, bf16[2048,768]{1,0:T(8,128)(2,1)} %param.15, bf16[3072,384]{1,0:T(8,128)(2,1)} %bitcast.127, bf16[3072,384]{1,0:T(8,128)(2,1)} %bitcast.125), kind=kOutput, calls=%fused_computation.140 | convolution fusion | flops 9811522560 | bytes 45631488 | tf_op jit(solution)/shard_map/dot_general | solution.py:194
  246.3 14.7 %convolution_convert_fusion.1 = bf16[768,3072]{1,0:T(8,128)(2,1)} fusion(bf16[2048,3072]{1,0:T(8,128)(2,1)} %get-tuple-element.134, f32[2048,768]{0,1:T(8,128)S(1)} %bitcast.88, f32[768]{0:T(1024)S(1)} %copy-done.31, f32[768]{0:T(1024)S(1)} %copy-done.25, f32[2048]{0:T(1024)S(1)} %add_rsqrt_fusion, f32[2048]{0:T(1024)S(1)} %broadcast_multiply_fusion.4), kind=kOutput, calls=%fused_computation.45 | convolution fusion | flops 9673900032 | bytes 23615488 | tf_op jit(solution)/shard_map/dot_general | solution.py:194
  260.9 14.3 %fusion.46 = (bf16[768]{0:T(1024)(128)(2,1)S(1)}, f32[2048,768]{1,0:T(8,128)}) fusion(bf16[2048,3072]{1,0:T(8,128)(2,1)S(1)} %copy-done.33, bf16[768,3072]{1,0:T(8,128)(2,1)} %constant_dynamic-update-slice_fusion.12), kind=kOutput, calls=%fused_computation.139 | convolution fusion | flops 9665248256 | bytes 23594496 | tf_op jit(solution)/shard_map/dot_general | solution.py:194
  275.2 6.7 copy.41
  281.9 6.6 multiply_reduce_fusion
  289.6 4.4 convert_reduce_fusion.1
  294.1 2.7 convolution_convert_fusion.4
  297.2 4.1 convolution_convert_fusion.3.g_ref
  302.1 1.2 copy-done.6
  303.3 13.5 %convolution_convert_fusion = bf16[3072,768]{1,0:T(8,128)(2,1)S(1)} fusion(bf16[2048,3072]{1,0:T(8,128)(2,1)} %get-tuple-element.127, bf16[2048,768]{1,0:T(8,128)(2,1)S(1)} %copy-done.6), kind=kOutput, calls=%fused_computation.44 | convolution fusion | flops 9666035712 | bytes 20447232 | tf_op jit(solution)/shard_map/dot_general | solution.py:194
  319.2 5.1 pad_maximum_fusion
  324.3 69.8 %attn_bwd.1 = (bf16[2048,768]{1,0:T(8,128)(2,1)}, bf16[2048,768]{1,0:T(8,128)(2,1)}, bf16[2048,768]{1,0:T(8,128)(2,1)}) custom-call(s32[1]{0:T(128)} %bitcast.seq_ref, bf16[2048,2304]{1,0:T(8,128)(2,1)} %add_convert_fusion.q_ref.k_ref.v_ref, bf16[2048,2304]{1,0:T(8,128)(2,1)} %add_convert_fusion.q_ref.k_ref.v_ref, ...), custom_call_target="tpu_custom_call" | custom-call | tf_op jit(solution)/shard_map/attn_bwd/pallas_call | solution.py:167
  394.1 2.2 constant_dynamic-update-slice_fusion.34
  398.1 3.6 copy-done.5
  401.6 9.4 %fusion.45 = (bf16[768]{0:T(1024)(128)(2,1)S(1)}, f32[2048,768]{1,0:T(8,128)}) fusion(bf16[2048,2304]{1,0:T(8,128)(2,1)S(1)} %constant_dynamic-update-slice_fusion.32, bf16[768,2304]{1,0:T(8,128)(2,1)S(1)} %copy-done.19), kind=kOutput, calls=%fused_computation.138 | convolution fusion | flops 7249329152 | bytes 19269120 | tf_op jit(solution)/shard_map/dot_general | solution.py:194
  411.1 5.2 reduce
  416.3 13.1 %convolution_convert_fusion.2 = bf16[768,2304]{1,0:T(8,128)(2,1)} fusion(bf16[2048,2304]{1,0:T(8,128)(2,1)} %copy-done.5, bf16[2048,768]{0,1:T(8,128)(2,1)S(1)} %copy-done.1, f32[768]{0:T(1024)S(1)} %copy-done.30, f32[768]{0:T(1024)S(1)} %copy-done.24, f32[2048]{0:T(1024)S(1)} %copy-done.21, f32[2048]{0:T(1024)S(1)} %copy-done.17), kind=kOutput, calls=%fused_computation.46 | convolution fusion | flops 7258963968 | bytes 16144384 | tf_op jit(solution)/shard_map/dot_general | solution.py:194
  429.4 6.5 copy.42
  436.0 4.5 fusion.22
  441.4 2.3 fusion.39
  443.8 2.8 maximum_maximum_fusion
  447.4 7.8 %fusion.21 = f32[2048,768]{0,1:T(8,128)} fusion(f32[2048,768]{0,1:T(8,128)} %copy-done.4, bf16[2048,768]{0,1:T(8,128)(2,1)S(1)} %copy-done.1, f32[2048,768]{0,1:T(8,128)} %copy.42, f32[2048]{0:T(1024)S(1)} %broadcast_multiply_fusion, f32[2048]{0:T(1024)S(1)} %broadcast_multiply_fusion.1, f32[768]{0:T(1024)S(1)} %copy-done.24, f32[2048]{0:T(1024)S(1)} %copy-done.21, ...), kind=kLoop, calls=%fused_computation.31 | loop fusion | flops 14155776 | bytes 22055936 | tf_op jit(solution)/shard_map/add | solution.py:335
  455.2 6.6 copy.46
  461.7 15.3 %add_convert_fusion.1 = bf16[2048,768]{0,1:T(8,128)(2,1)S(1)} fusion(f32[2048,768]{0,1:T(8,128)} %copy-done.2, bf16[2048,3072]{1,0:T(8,128)(2,1)} %get-tuple-element.127, f32[768]{0:T(1024)S(1)} %reshape.311, bf16[3072,384]{1,0:T(8,128)(2,1)} %bitcast.128, bf16[3072,384]{1,0:T(8,128)(2,1)} %bitcast.126), kind=kOutput, calls=%fused_computation.38 | convolution fusion | flops 9677832192 | bytes 26741760 | tf_op jit(solution)/shard_map/dot_general | solution.py:194
  477.1 2.8 copy.45
  479.9 127.8 %reduce-scatter.3.cloned.1.call-done = bf16[160,384]{1,0:T(8,128)(2,1)} async-done(((bf16[5120,384]{1,0:T(8,128)(2,1)}), bf16[160,384]{1,0:T(8,128)(2,1)}) %reduce-scatter.3.cloned.1.call-update) | async-done | bytes 122896 | tf_op jit(solution)/shard_map/reduce_scatter | solution.py:284
  611.6 143.1 %reduce-scatter.5.cloned.1.call-done = bf16[432,384]{1,0:T(8,128)(2,1)} async-done(((bf16[13824,384]{1,0:T(8,128)(2,1)}), bf16[432,384]{1,0:T(8,128)(2,1)}) %reduce-scatter.5.cloned.1.call-update) | async-done | bytes 331792 | tf_op jit(solution)/shard_map/reduce_scatter | solution.py:284
  754.7 1.5 fusion.41
  757.0 1.6 slice_convert_fusion
  (168 shorter events, 34.8 us)
Async XLA Ops:
  7.2 67.9 %all-gather.3.cloned.1.call-start = ((), (), s32[]{:S(2)}) async-start(), calls=%async_computation.2 | async-start | bytes 4055040 | tf_op jit(solution)/shard_map/all_gather | solution.py:229
  9.7 154.8 %all-gather.5.cloned.1.call-start = ((), (), s32[]{:S(2)}) async-start(), calls=%async_computation.3 | async-start | bytes 10948608 | tf_op jit(solution)/shard_map/all_gather | solution.py:229
  14.5 0.7 copy-start.15
  15.3 592.3 %reduce-scatter.3.cloned.1.call-start = ((), (), s32[]{:S(2)}) async-start(), calls=%async_computation.4 | async-start | bytes 4055040 | tf_op jit(solution)/shard_map/reduce_scatter | solution.py:284
  18.5 154.8 %copy-start = (bf16[2048,768]{0,1:T(8,128)(2,1)}, bf16[2048,768]{0,1:T(8,128)(2,1)S(1)}, u32[]{:S(2)}) copy-start(bf16[2048,768]{0,1:T(8,128)(2,1)S(1)} %copy.37) | copy-start | bytes 9437188
  27.7 62.8 %copy-start.16 = (f32[2048]{0:T(1024)}, f32[2048]{0:T(1024)S(1)}, u32[]{:S(2)}) copy-start(f32[2048]{0:T(1024)S(1)} %broadcast_multiply_fusion.5) | copy-start | bytes 24580
  28.5 61.9 %copy-start.20 = (f32[2048]{0:T(1024)}, f32[2048]{0:T(1024)S(1)}, u32[]{:S(2)}) copy-start(f32[2048]{0:T(1024)S(1)} %add_rsqrt_fusion.1) | copy-start | bytes 24580
  87.5 3.0 copy-start.23
  87.5 3.0 copy-start.27
  87.5 3.0 copy-start.29
  90.5 11.1 %copy-start.18 = (bf16[768,2304]{1,0:T(8,128)(2,1)}, bf16[768,2304]{1,0:T(8,128)(2,1)S(1)}, u32[]{:S(2)}) copy-start(bf16[768,2304]{1,0:T(8,128)(2,1)S(1)} %constant_dynamic-update-slice_fusion) | copy-start | bytes 10616836
  167.8 8.8 %copy-start.11 = (bf16[1,16,48,384]{3,2,1,0:T(8,128)(2,1)}, bf16[1,16,48,384]{3,2,1,0:T(8,128)(2,1)S(1)}, u32[]{:S(2)}) copy-start(bf16[1,16,48,384]{3,2,1,0:T(8,128)(2,1)S(1)} %get-tuple-element.74) | copy-start | bytes 1769476
  167.8 8.8 %copy-start.13 = (bf16[1,16,48,384]{3,2,1,0:T(8,128)(2,1)}, bf16[1,16,48,384]{3,2,1,0:T(8,128)(2,1)S(1)}, u32[]{:S(2)}) copy-start(bf16[1,16,48,384]{3,2,1,0:T(8,128)(2,1)S(1)} %get-tuple-element.75) | copy-start | bytes 1769476
  167.8 5.5 copy-start.9
  167.8 5.5 copy-start.32
  176.6 6.8 copy-start.2
  177.3 8.0 %copy-start.25 = (f32[768]{0:T(1024)S(1)}, f32[768]{0:T(1024)}, u32[]{:S(2)}) copy-start(f32[768]{0:T(1024)} %reshape.308) | copy-start | bytes 9220
  177.3 8.0 %copy-start.31 = (f32[768]{0:T(1024)S(1)}, f32[768]{0:T(1024)}, u32[]{:S(2)}) copy-start(f32[768]{0:T(1024)} %reshape.309) | copy-start | bytes 9220
  185.3 61.0 %slice-start = ((s8[6291456]{0:T(1024)(128)(4,1)}), s8[2097152]{0:T(1024)(128)(4,1)S(1)}, s32[]{:S(2)}) async-start(s8[6291456]{0:T(1024)(128)(4,1)} %bitcast.87), calls=%async_computation.6 | async-start | bytes 4194304
  212.4 33.9 %slice-start.1 = ((s8[6291456]{0:T(1024)(128)(4,1)}), s8[4194304]{0:T(1024)(128)(4,1)S(1)}, s32[]{:S(2)}) async-start(s8[6291456]{0:T(1024)(128)(4,1)} %bitcast.87), calls=%async_computation.7 | async-start | bytes 8388608
  246.2 14.7 %copy-start.33 = (bf16[2048,3072]{1,0:T(8,128)(2,1)S(1)}, bf16[2048,3072]{1,0:T(8,128)(2,1)}, u32[]{:S(2)}) copy-start(bf16[2048,3072]{1,0:T(8,128)(2,1)} %get-tuple-element.134) | copy-start | bytes 37748740
  275.2 13.3 %slice-start.2 = ((s8[6291456]{0:T(1024)(128)(4,1)}), s8[2097152]{0:T(1024)(128)(4,1)S(1)}, s32[]{:S(2)}) async-start(s8[6291456]{0:T(1024)(128)(4,1)} %bitcast.89), calls=%async_computation.8 | async-start | bytes 4194304
  281.9 6.6 slice-start.3
  281.9 7.7 %copy-start.3 = (f32[2048,768]{0,1:T(8,128)S(1)}, f32[2048,768]{0,1:T(8,128)}, u32[]{:S(2)}) copy-start(f32[2048,768]{0,1:T(8,128)} %copy.41) | copy-start | bytes 18874372
  289.6 4.4 copy-start.10
  294.0 3.2 copy-start.4
  294.1 3.2 copy-start.12
  294.1 3.2 copy-start.14
  294.1 7.3 slice-start.4
  297.2 4.1 slice-start.5
  301.4 1.9 copy-start.6
  394.1 2.8 copy-start.8
  394.1 3.8 copy-start.7
  396.9 4.7 copy-start.19
  398.1 3.6 copy-start.5
  411.0 5.2 copy-start.1
  411.1 5.2 copy-start.17
  411.1 5.2 copy-start.21
  411.1 5.2 copy-start.24
  411.1 5.2 copy-start.30
  435.9 5.1 copy-start.28
  436.0 5.2 copy-start.26
  446.5 0.7 copy-start.22
  446.6 308.2 %reduce-scatter.5.cloned.1.call-start = ((), (), s32[]{:S(2)}) async-start(), calls=%async_computation.5 | async-start | bytes 10948608 | tf_op jit(solution)/shard_map/reduce_scatter | solution.py:284
Sparse Core Ops, SparseCore 0:
  11.5 63.6 all-gather.2
  78.6 85.7 all-gather.4
  446.7 160.9 reduce-scatter.2
  613.6 141.1 reduce-scatter.4
